TPU v7x, 32 devices: a whole 2x2x4 slice. The times are simulated.
32 devices in a mesh: heads: 4 (over x, core), ctx: 8 (over z, y).
Axes of the slice: x: 2, y: 2, z: 4, core: 2. Of those that a mesh axis runs over, the one named last changes fastest.
Arguments:
- queries: bfloat16 [1536, 2048], P('ctx', 'heads'), may hold values from -6 to 6
- key_states: bfloat16 [1536, 512], P('ctx', 'heads'), may hold values from -6 to 6
- value_states: bfloat16 [1536, 512], P('ctx', 'heads'), may hold values from -6 to 6
- attention_out: bfloat16 [1536, 2048], P('ctx', 'heads'), may hold values from -2 to 2
- out_grad: bfloat16 [1536, 2048], P('ctx', 'heads'), may hold values from -6 to 6
- log_sum_exp: float32 [16, 1536], P('heads', 'ctx'), may hold values from 0 to 16, as said below
- block_counts: int32 [8], replicated, may hold values from 1 to 3, as said below
- w_query: bfloat16 [4096, 2048], P(None, 'heads'), may hold values from -0.09375 to 0.09375
- w_key: bfloat16 [4096, 512], P(None, 'heads'), may hold values from -0.09375 to 0.09375
- w_value: bfloat16 [4096, 512], P(None, 'heads'), may hold values from -0.09375 to 0.09375
Outputs:
- input_grad: bfloat16 [1536, 4096], P('ctx', 'heads')
- key_grad: float32 [1536, 512], P('ctx', 'heads')
- value_grad: float32 [1536, 512], P('ctx', 'heads')
Inputs may be any that keep to these rules, and one draw needn't show every extreme that they name: `block_counts`: one entry equals 3. `log_sum_exp`: finite offsets of each row's scores.
All inputs are finite; a program needn't handle non-finite values.
Results may differ from a plain program's by a relative error of at most 0.0063.
Values may be sent and summed in bfloat16 or wider, within the bound.
A program may use at most 128 MiB of HBM per device.

v0:
```python
import functools
import math

import jax
import jax.numpy as jnp
from jax import lax
from jax.experimental import pallas as pl
from jax.experimental.pallas import tpu as pltpu
from jax.sharding import PartitionSpec as P

BLOCK = 64
LOG2E = math.log2(math.e)
F32 = jnp.float32
BF16 = jnp.bfloat16
NT = (((1,), (1,)), ((), ()))
TN = (((0,), (0,)), ((), ()))


def dot(a, b, dims=(((1,), (0,)), ((), ()))):
    return lax.dot_general(a, b, dims, preferred_element_type=F32)


def kernel(
    zs, nx, ns,
    q_hbm, k_hbm, v_hbm, o_hbm, do_hbm, lse_hbm, cnt_hbm, wq_hbm, wk_hbm, wv_hbm,
    out_ref, dk_ref, dv_ref,
    cnt_ref, q_ref, k_ref, v_ref, o_ref, do_ref, lse_ref, pair_q, pair_do, wq, wkv, qs, dos, lse2, delta, dqt,
    dq_own, dq_send, dq_recv, gq, gkv, acc, kv, part, fsend, frcv, keep, hold, csend, crcv, tsend, trcv, xsend, xrcv,
    in_sem, w_sem, own_send, kv_recv, swap_send, swap_recv, f_send, f_recv,
    c_send, c_recv, t_send, t_recv, x_send, x_recv,
):
    cap, dim = k_ref.shape
    group = q_ref.shape[1] // dim
    half = cap // 2
    np = cap // half
    scale = 1.0 / math.sqrt(dim)
    me = lax.axis_index("ctx")
    y = lax.rem(me, 2)
    z = lax.div(me, 2)
    pair = me + 1 - 2 * y
    h = lax.axis_index("heads")
    core = lax.rem(h, 2)
    x = lax.div(h, 2)
    other = h + 1 - 2 * core
    across = [2 * lax.rem(x + dx, nx) + core for dx in range(nx)]

    in_copies = [
        pltpu.make_async_copy(src, dst, in_sem.at[i])
        for i, (src, dst) in enumerate((
            (k_hbm, k_ref), (v_hbm, v_ref), (q_hbm, q_ref), (do_hbm, do_ref), (o_hbm, o_ref),
            (lse_hbm, lse_ref), (cnt_hbm, cnt_ref),
        ))
    ]
    for copy in in_copies:
        copy.start()
    w_copies = [
        pltpu.make_async_copy(wq_hbm, wq, w_sem.at[0]),
        pltpu.make_async_copy(wk_hbm, wkv.at[:, pl.ds(0, dim)], w_sem.at[1]),
        pltpu.make_async_copy(wv_hbm, wkv.at[:, pl.ds(dim, dim)], w_sem.at[2]),
    ]

    def remote(src, dst, send, recv, **device):
        return pltpu.make_async_remote_copy(
            src_ref=src, dst_ref=dst, send_sem=send, recv_sem=recv,
            device_id=device, device_id_type=pl.DeviceIdType.MESH,
        )

    barrier = pltpu.get_barrier_semaphore()

    def greet(**device):
        pl.semaphore_signal(
            barrier, inc=1, device_id=device, device_id_type=pl.DeviceIdType.MESH
        )

    def greet_line(z2, _):
        @pl.when(z2 != z)
        def _():
            greet(ctx=2 * z2 + y)
        return 0

    lax.fori_loop(0, zs, greet_line, 0)
    greet(ctx=pair)
    greet(heads=other)
    for dx in range(1, nx):
        greet(heads=across[dx])
    for copy in in_copies:
        copy.wait()
    for copy in w_copies:
        copy.start()
    with jax.named_scope("barrier"):
        pl.semaphore_wait(barrier, zs + nx)

    own = (k_ref, v_ref)

    def own_copy(t, z2):
        return remote(own[t], kv.at[t, z], own_send.at[t, z2], kv_recv.at[t, z], ctx=2 * z2 + y)

    def arrived(z1):
        for t in range(2):
            remote(
                kv.at[t, z1], kv.at[t, z1], own_send.at[t, z1], kv_recv.at[t, z1], ctx=pair
            ).wait_recv()

    swaps = [
        remote(src, dst, swap_send.at[i], swap_recv.at[i], ctx=pair)
        for i, (src, dst) in enumerate((
            (q_ref, pair_q), (do_ref, pair_do), (lse2.at[0], lse2.at[1]), (delta.at[0], delta.at[1]),
            *((dq_send.at[r], dq_recv.at[r]) for r in range(np)),
        ))
    ]

    def fin_copy(r, z1):
        return remote(
            fsend.at[r, z1], frcv.at[r, z], f_send.at[r, z1], f_recv.at[r, z], ctx=2 * z1 + y
        )

    def fin_wait(r, z2):
        remote(
            fsend.at[r, z2], frcv.at[r, z2], f_send.at[r, z2], f_recv.at[r, z2], ctx=2 * z2 + y
        ).wait_recv()

    swaps[0].start()
    swaps[1].start()

    def push_own(i, _):
        z2 = zs - 1 - i

        @pl.when(z2 > z)
        def _():
            for t in range(2):
                own_copy(t, z2).start()
        return 0

    lax.fori_loop(0, zs, push_own, 0)

    lane = lax.broadcasted_iota(jnp.int32, (1, group * cap), 1)
    row = lax.rem(lane, cap)
    alive = row < cnt_ref[me] * BLOCK
    prod = jnp.concatenate(
        [
            do_ref[:, g * dim:(g + 1) * dim].astype(F32) * o_ref[:, g * dim:(g + 1) * dim].astype(F32)
            for g in range(group)
        ],
        axis=0,
    )
    delta[0] = lax.dot_general(
        jnp.ones((8, dim), F32), prod, NT,
        preferred_element_type=F32, precision=lax.Precision.HIGHEST,
    )[0:1]
    lse_row = jnp.concatenate([lse_ref[g:g + 1, :] for g in range(group)], axis=1)
    lse2[0] = jnp.where(alive, lse_row * LOG2E, 1e30)

    def stack(who, q, do):
        for g in range(group):
            cols = slice(g * dim, (g + 1) * dim)
            qs[who, g * cap:(g + 1) * cap, :] = q[:, cols]
            dos[who, g * cap:(g + 1) * cap, :] = do[:, cols]

    stack(0, q_ref, do_ref)
    swaps[2].start()
    swaps[3].start()
    key_row = lax.broadcasted_iota(jnp.int32, (cap, group * cap), 0)

    def tile(who, key, value, b, diagonal):
        scores = dot(key, qs[who], NT)
        prob_grad = dot(value, dos[who], NT)
        visible = key_row < cnt_ref[b] * BLOCK
        if diagonal:
            visible = visible & (key_row <= row)
        prob = jnp.where(visible, jnp.exp2(scores * (scale * LOG2E) - lse2[who]), 0.0)
        grad = (prob * (prob_grad - delta[who])).astype(BF16)
        d_value = dot(prob.astype(BF16), dos[who])
        d_key = dot(grad, qs[who])
        terms = dot(key, grad, TN)
        if diagonal:
            dqt[who] = terms
        else:
            dqt[who] += terms
        return d_key, d_value

    with jax.named_scope("diag"):
        d_key, d_value = tile(0, k_ref[...], v_ref[...], me, True)
        acc[0] = d_key
        acc[1] = d_value
    dqt[1] = jnp.zeros_like(dqt[1])

    def own_step(z1, _):
        @pl.when(z1 < z)
        def _():
            with jax.named_scope("wait_kv"):
                arrived(z1)
            with jax.named_scope("own_tile"):
                d_key, d_value = tile(0, kv[0, z1], kv[1, z1], 2 * z1 + y, False)
                part[z1, 0] = d_key
                part[z1, 1] = d_value
        return 0

    lax.fori_loop(0, zs, own_step, 0)
    with jax.named_scope("wait_swap"):
        for copy in swaps[:4]:
            copy.wait_recv()
    stack(1, pair_q, pair_do)

    def pair_step(z1, _):
        @pl.when(z1 < z)
        def _():
            with jax.named_scope("pair_tile"):
                d_key, d_value = tile(1, kv[0, z1], kv[1, z1], 2 * z1 + y, False)
                d_key = (part[z1, 0] + d_key).astype(BF16)
                d_value = (part[z1, 1] + d_value).astype(BF16)
                for r in range(np):
                    fsend[r, z1, 0] = d_key[r * half:(r + 1) * half]
                    fsend[r, z1, 1] = d_value[r * half:(r + 1) * half]
            fin_copy(0, z1).start()
        return 0

    lax.fori_loop(0, zs, pair_step, 0)

    def later(i, _):
        r = lax.div(i, zs) + 1
        z1 = lax.rem(i, zs)

        @pl.when(z1 < z)
        def _():
            fin_copy(r, z1).start()
        return 0

    lax.fori_loop(0, zs * (np - 1), later, 0)

    @pl.when(y == 0)
    def _():
        with jax.named_scope("pair_own"):
            d_key, d_value = tile(1, k_ref[...], v_ref[...], me, False)
            acc[0] += d_key
            acc[1] += d_value

    pair_dq = jnp.transpose(dqt[1]).astype(BF16)
    for r in range(np):
        for g in range(group):
            dq_send[r, g] = pair_dq[g * cap + r * half:g * cap + (r + 1) * half]
        swaps[4 + r].start()
    dq_own[...] = jnp.transpose(dqt[0])
    for copy in w_copies:
        copy.wait()
    width = hold.shape[2]

    def whole(owner, s, rows):
        cols = pl.ds(pl.multiple_of((owner * ns + s) * width, width), width)
        return dot(gq[rows, :], wq[cols, :], NT) + dot(gkv[rows, :], wkv[cols, :], NT)

    def chip_copy(s):
        return remote(csend.at[s], crcv.at[s], c_send.at[s], c_recv.at[s], heads=other)

    def near_copy(dx, r, s):
        at = (dx, r, s)
        return remote(tsend.at[at], trcv.at[at], t_send.at[at], t_recv.at[at], heads=other)

    def cross_copy(dx, r, s):
        at = (dx, r, s)
        return remote(xsend.at[at], xrcv.at[at], x_send.at[at], x_recv.at[at], heads=across[dx])

    def cross(dx, r, s):
        with jax.named_scope("wait_near"):
            near_copy(dx, r, s).wait_recv()
        xsend[dx, r, s] = (keep[s] + trcv[dx, r, s].astype(F32)).astype(BF16)
        cross_copy(dx, r, s).start()

    for r in range(np):
        rows = slice(r * half, (r + 1) * half)

        def collect(i, _):
            z2 = zs - 1 - i

            @pl.when(z2 > z)
            def _():
                fin_wait(r, z2)
                acc[:, rows, :] += frcv[r, z2].astype(F32)
            return 0

        with jax.named_scope("wait_dq"):
            swaps[4 + r].wait_recv()
        for g in range(group):
            total = dq_own[g * cap + r * half:g * cap + (r + 1) * half, :] + dq_recv[r, g].astype(F32)
            gq[rows, g * dim:(g + 1) * dim] = (total * scale).astype(BF16)
        with jax.named_scope("collect"):
            lax.fori_loop(0, zs, collect, 0)
        key_total = acc[0, rows, :] * scale
        value_total = acc[1, rows, :]
        dk_ref[rows, :] = key_total
        dv_ref[rows, :] = value_total
        gkv[rows, 0:dim] = key_total.astype(BF16)
        gkv[rows, dim:2 * dim] = value_total.astype(BF16)
        for dx in range(1, nx):
            for s in range(ns):
                tsend[dx, r, s] = whole(across[dx] + 1 - 2 * core, s, rows).astype(BF16)
                near_copy(dx, r, s).start()
            for s in range(ns):
                keep[s] = whole(across[dx], s, rows)
                cross(dx, r, s)
    everything = slice(0, cap)
    for s in range(ns):
        csend[s] = whole(other, s, everything).astype(BF16)
        chip_copy(s).start()
    for s in range(ns):
        hold[s] = whole(h, s, everything)
    for s in range(ns):
        chip_copy(s).wait_recv()
        hold[s] += crcv[s].astype(F32)
    for r in range(np):
        rows = slice(r * half, (r + 1) * half)
        for s in range(ns):
            total = hold[s, rows, :]
            for dx in range(1, nx):
                with jax.named_scope("wait_cross"):
                    cross_copy(dx, r, s).wait_recv()
                total = total + xrcv[dx, r, s].astype(F32)
            out_ref[rows, s * width:(s + 1) * width] = total.astype(BF16)

    for copy in swaps:
        copy.wait_send()

    def drain(z2, _):
        @pl.when(z2 > z)
        def _():
            for t in range(2):
                own_copy(t, z2).wait_send()

        @pl.when(z2 < z)
        def _():
            for r in range(np):
                fin_copy(r, z2).wait_send()
        return 0

    lax.fori_loop(0, zs, drain, 0)
    for s in range(ns):
        chip_copy(s).wait_send()
        for dx in range(1, nx):
            for r in range(np):
                near_copy(dx, r, s).wait_send()
                cross_copy(dx, r, s).wait_send()


def on_device(
    n, nh, queries, key_states, value_states, attention_out, out_grad, log_sum_exp, block_counts,
    w_query, w_key, w_value,
):
    zs, nx, ns = n // 2, nh // 2, 4
    cap, dim = key_states.shape
    width = queries.shape[1]
    rows = width // dim * cap
    model = w_query.shape[0]
    mine = model // nh
    chunk = mine // ns
    vmem = pl.BlockSpec(memory_space=pltpu.VMEM)
    half = cap // 2
    np = cap // half
    hbm = pl.BlockSpec(memory_space=pltpu.HBM)
    dma = pltpu.SemaphoreType.DMA
    results = pl.pallas_call(
        functools.partial(kernel, zs, nx, ns),
        out_shape=(
            jax.ShapeDtypeStruct((cap, mine), BF16),
            jax.ShapeDtypeStruct((cap, dim), F32),
            jax.ShapeDtypeStruct((cap, dim), F32),
        ),
        in_specs=[hbm] * 10,
        out_specs=(vmem, vmem, vmem),
        scratch_shapes=[
            pltpu.SMEM(block_counts.shape, jnp.int32),
            pltpu.VMEM((cap, width), BF16),
            pltpu.VMEM((cap, dim), BF16),
            pltpu.VMEM((cap, dim), BF16),
            pltpu.VMEM((cap, width), BF16),
            pltpu.VMEM((cap, width), BF16),
            pltpu.VMEM(log_sum_exp.shape, F32),
            pltpu.VMEM((cap, width), BF16),
            pltpu.VMEM((cap, width), BF16),
            pltpu.VMEM((model, width), BF16),
            pltpu.VMEM((model, 2 * dim), BF16),
            pltpu.VMEM((2, rows, dim), BF16),
            pltpu.VMEM((2, rows, dim), BF16),
            pltpu.VMEM((2, 1, rows), F32),
            pltpu.VMEM((2, 1, rows), F32),
            pltpu.VMEM((2, dim, rows), F32),
            pltpu.VMEM((rows, dim), F32),
            pltpu.VMEM((np, width // dim, half, dim), BF16),
            pltpu.VMEM((np, width // dim, half, dim), BF16),
            pltpu.VMEM((cap, width), BF16),
            pltpu.VMEM((cap, 2 * dim), BF16),
            pltpu.VMEM((2, cap, dim), F32),
            pltpu.VMEM((2, zs, cap, dim), BF16),
            pltpu.VMEM((zs, 2, cap, dim), F32),
            pltpu.VMEM((np, zs, 2, half, dim), BF16),
            pltpu.VMEM((np, zs, 2, half, dim), BF16),
            pltpu.VMEM((ns, half, chunk), F32),
            pltpu.VMEM((ns, cap, chunk), F32),
            pltpu.VMEM((ns, cap, chunk), BF16),
            pltpu.VMEM((ns, cap, chunk), BF16),
            pltpu.VMEM((nx, np, ns, half, chunk), BF16),
            pltpu.VMEM((nx, np, ns, half, chunk), BF16),
            pltpu.VMEM((nx, np, ns, half, chunk), BF16),
            pltpu.VMEM((nx, np, ns, half, chunk), BF16),
            dma((7,)),
            dma((3,)),
            dma((2, zs)),
            dma((2, zs)),
            dma((4 + np,)),
            dma((4 + np,)),
            dma((np, zs)),
            dma((np, zs)),
            dma((ns,)),
            dma((ns,)),
            dma((nx, np, ns)),
            dma((nx, np, ns)),
            dma((nx, np, ns)),
            dma((nx, np, ns)),
        ],
        compiler_params=pltpu.CompilerParams(
            collective_id=0, has_side_effects=True, vmem_limit_bytes=52 * 1024 * 1024
        ),
    )(
        *(
            pltpu.with_memory_space_constraint(a, pltpu.HBM)
            for a in (
                queries, key_states, value_states, attention_out, out_grad, log_sum_exp,
                block_counts, w_query, w_key, w_value,
            )
        )
    )
    return results


def solution(mesh):
    return jax.shard_map(
        functools.partial(on_device, mesh.shape["ctx"], mesh.shape["heads"]),
        mesh=mesh,
        in_specs=(
            P("ctx", "heads"),
            P("ctx", "heads"),
            P("ctx", "heads"),
            P("ctx", "heads"),
            P("ctx", "heads"),
            P("heads", "ctx"),
            P(),
            P(None, "heads"),
            P(None, "heads"),
            P(None, "heads"),
        ),
        out_specs=(P("ctx", "heads"), P("ctx", "heads"), P("ctx", "heads")),
        check_vma=False,
    )
```

profile of v0, /device:TPU:0, one launch (start us, length us, event | category | flops | bytes accessed | tf_op | source)
XLA Modules:
  0.0 38.4 jit_solution(10806331241256708731)
XLA Ops:
  0.6 35.7 %shard_map.121 = (bf16[192,1024]{1,0:T(8,128)(2,1)S(1)}, f32[192,128]{1,0:T(8,128)S(1)}, f32[192,128]{1,0:T(8,128)S(1)}) custom-call(bf16[192,512]{1,0:T(8,128)(2,1)} %q_hbm.1, bf16[192,128]{1,0:T(8,128)(2,1)} %k_hbm.1, bf16[192,128]{1,0:T(8,128)(2,1)} %v_hbm.1, bf16[192,512]{1,0:T(8,128)(2,1)} %o_hbm.1, bf16[192,512]{1,0:T(8,128)(2,1)} %do_hbm.1, ...), custom_call_target="tpu_custom_call" | custom-call | tf_op jit(solution)/shard_map/pallas_call | solution.py:359
  36.3 0.7 %copy.16 = bf16[192,1024]{1,0:T(8,128)(2,1)} copy(bf16[192,1024]{1,0:T(8,128)(2,1)S(1)} %get-tuple-element.6) | data formatting | bytes 786432
  37.1 0.6 %copy.17 = f32[192,128]{1,0:T(8,128)} copy(f32[192,128]{1,0:T(8,128)S(1)} %get-tuple-element.7) | data formatting | bytes 196608
  37.7 0.6 %copy.18 = f32[192,128]{1,0:T(8,128)} copy(f32[192,128]{1,0:T(8,128)S(1)} %get-tuple-element.8) | data formatting | bytes 196608
where the time goes:
time: 38.5 us; the launch traced here: 38.4 us
  Pallas kernels  35.7 us (93%)
  local copies, waits for them, and re-layouts  2.03 us (5%)
  between operations  0.64 us (2%)
    pallas_call x1, Pallas kernels, on_device(): pl.pallas_call(functools.partial(kernel, zs, nx, ns), out_shape=(jax.Shap...  35.7 us
    unnamed x3, local copies, waits for them, and re-layouts  2.03 us

commit v1 on v0

v1 whole, which is shorter than its diff:
```python
import functools
import math

import jax
import jax.numpy as jnp
from jax import lax
from jax.experimental import pallas as pl
from jax.experimental.pallas import tpu as pltpu
from jax.sharding import PartitionSpec as P

BLOCK = 64
LOG2E = math.log2(math.e)
F32 = jnp.float32
BF16 = jnp.bfloat16
NT = (((1,), (1,)), ((), ()))
TN = (((0,), (0,)), ((), ()))


def dot(a, b, dims=(((1,), (0,)), ((), ()))):
    return lax.dot_general(a, b, dims, preferred_element_type=F32)


def row_blocks(np, ns):
    plan = []
    for r in range(np):
        if r == 0:
            plan.append(((0, 1), (1, 1), (2, ns - 2)))
        elif r == np - 1:
            plan.append(((0, ns - 2), (ns - 2, 1), (ns - 1, 1)))
        else:
            plan.append(((0, ns // 2), (ns // 2, ns - ns // 2)))
    return plan


def kernel(
    zs, nx, ns, nb,
    q_hbm, k_hbm, v_hbm, o_hbm, do_hbm, lse_hbm, cnt_hbm, wq_hbm, wk_hbm, wv_hbm,
    out_ref, dk_ref, dv_ref,
    cnt_ref, own, qd, o_ref, lse_ref, pair_qd, wq, wkv, qs, dos, stats, dqt,
    dq_own, dq_send, dq_recv, gq, gkv, acc, kv, part, fsend, frcv, keep, hold, csend, crcv, tsend, trcv, xsend, xrcv,
    in_sem, w_sem, own_send, kv_recv, swap_send, swap_recv, f_send, f_recv,
    c_send, c_recv, t_send, t_recv, x_send, x_recv,
):
    cap, dim = own.shape[1:]
    group = qd.shape[2] // dim
    np = dq_send.shape[0]
    half = cap // np
    scale = 1.0 / math.sqrt(dim)
    plan = row_blocks(np, ns)
    first = [sum(len(p) for p in plan[:r]) for r in range(np)]
    me = lax.axis_index("ctx")
    y = lax.rem(me, 2)
    z = lax.div(me, 2)
    pair = me + 1 - 2 * y
    h = lax.axis_index("heads")
    core = lax.rem(h, 2)
    x = lax.div(h, 2)
    other = h + 1 - 2 * core
    across = [2 * lax.rem(x + dx, nx) + core for dx in range(nx)]

    loads = [
        pltpu.make_async_copy(src, dst, in_sem.at[i])
        for src, dst, i in (
            (k_hbm, own.at[0], 0), (v_hbm, own.at[1], 0), (q_hbm, qd.at[0], 1), (do_hbm, qd.at[1], 1),
            (o_hbm, o_ref, 2), (lse_hbm, lse_ref, 3), (cnt_hbm, cnt_ref, 4),
        )
    ]
    for copy in loads:
        copy.start()
    w_copies = [
        pltpu.make_async_copy(wq_hbm, wq, w_sem.at[0]),
        pltpu.make_async_copy(wk_hbm, wkv.at[:, pl.ds(0, dim)], w_sem.at[1]),
        pltpu.make_async_copy(wv_hbm, wkv.at[:, pl.ds(dim, dim)], w_sem.at[1]),
    ]

    def remote(src, dst, send, recv, **device):
        return pltpu.make_async_remote_copy(
            src_ref=src, dst_ref=dst, send_sem=send, recv_sem=recv,
            device_id=device, device_id_type=pl.DeviceIdType.MESH,
        )

    barrier = pltpu.get_barrier_semaphore()

    def greet(**device):
        pl.semaphore_signal(
            barrier, inc=1, device_id=device, device_id_type=pl.DeviceIdType.MESH
        )

    def greet_line(z2, _):
        @pl.when(z2 != z)
        def _():
            greet(ctx=2 * z2 + y)
        return 0

    lax.fori_loop(0, zs, greet_line, 0)
    greet(ctx=pair)
    greet(heads=other)
    for dx in range(1, nx):
        greet(heads=across[dx])
    pltpu.make_async_copy(own, own, in_sem.at[0]).wait()
    pltpu.make_async_copy(qd, qd, in_sem.at[1]).wait()
    for copy in loads[4:]:
        copy.wait()
    for copy in w_copies:
        copy.start()
    with jax.named_scope("barrier"):
        pl.semaphore_wait(barrier, zs + nx)

    def own_copy(z2):
        return remote(own, kv.at[z], own_send.at[z2], kv_recv.at[z], ctx=2 * z2 + y)

    pair_own_copy = remote(own, kv.at[zs], own_send.at[zs], kv_recv.at[zs], ctx=pair)

    def arrived(z1):
        remote(kv.at[z1], kv.at[z1], own_send.at[z1], kv_recv.at[z1], ctx=pair).wait_recv()

    swap_qd = remote(qd, pair_qd, swap_send.at[0], swap_recv.at[0], ctx=pair)
    swap_stats = remote(stats.at[0], stats.at[1], swap_send.at[1], swap_recv.at[1], ctx=pair)

    def swap_dq(r):
        return remote(dq_send.at[r], dq_recv.at[r], swap_send.at[2], swap_recv.at[2 + r], ctx=pair)

    def fin_copy(r, z1):
        return remote(
            fsend.at[z1, r], frcv.at[z, r], f_send.at[z1], f_recv.at[z, r], ctx=2 * z1 + y
        )

    def pair_fin(r):
        return remote(
            fsend.at[zs, r], frcv.at[zs, r], f_send.at[zs], f_recv.at[zs, r], ctx=pair
        )

    def fin_wait(r, z2):
        remote(
            fsend.at[z2, r], frcv.at[z2, r], f_send.at[z2], f_recv.at[z2, r], ctx=pair
        ).wait_recv()

    swapping = z > 0

    @pl.when(swapping)
    def _():
        swap_qd.start()

    @pl.when((z == 0) & (y == 0))
    def _():
        pair_own_copy.start()

    def push_own(i, _):
        z2 = zs - 1 - i

        @pl.when(z2 > z)
        def _():
            own_copy(z2).start()
        return 0

    lax.fori_loop(0, zs, push_own, 0)

    lane = lax.broadcasted_iota(jnp.int32, (1, group * cap), 1)
    row = lax.rem(lane, cap)
    alive = row < cnt_ref[me] * BLOCK
    prod = jnp.concatenate(
        [
            qd[1, :, g * dim:(g + 1) * dim].astype(F32) * o_ref[:, g * dim:(g + 1) * dim].astype(F32)
            for g in range(group)
        ],
        axis=0,
    )
    stats[0, 1:2] = lax.dot_general(
        jnp.ones((8, dim), F32), prod, NT,
        preferred_element_type=F32, precision=lax.Precision.HIGHEST,
    )[0:1]
    lse_row = jnp.concatenate([lse_ref[g:g + 1, :] for g in range(group)], axis=1)
    stats[0, 0:1] = jnp.where(alive, lse_row * LOG2E, 1e30)

    def stack(who, src):
        for g in range(group):
            cols = slice(g * dim, (g + 1) * dim)
            qs[who, g * cap:(g + 1) * cap, :] = src[0, :, cols]
            dos[who, g * cap:(g + 1) * cap, :] = src[1, :, cols]

    stack(0, qd)

    @pl.when(swapping)
    def _():
        swap_stats.start()

    key_row = lax.broadcasted_iota(jnp.int32, (cap, group * cap), 0)

    def tile(who, key, value, b, diagonal):
        scores = dot(key, qs[who], NT)
        prob_grad = dot(value, dos[who], NT)
        visible = key_row < cnt_ref[b] * BLOCK
        if diagonal:
            visible = visible & (key_row <= row)
        prob = jnp.where(visible, jnp.exp2(scores * (scale * LOG2E) - stats[who, 0:1]), 0.0)
        grad = (prob * (prob_grad - stats[who, 1:2])).astype(BF16)
        d_value = dot(prob.astype(BF16), dos[who])
        d_key = dot(grad, qs[who])
        terms = dot(key, grad, TN)
        if diagonal:
            dqt[who] = terms
        else:
            dqt[who] += terms
        return d_key, d_value

    with jax.named_scope("diag"):
        d_key, d_value = tile(0, own[0], own[1], me, True)
        acc[0] = d_key
        acc[1] = d_value

    def own_step(z1, _):
        @pl.when((z1 < z) | ((z1 == zs) & (z == 0) & (y == 1)))
        def _():
            with jax.named_scope("wait_kv"):
                arrived(z1)
            with jax.named_scope("own_tile"):
                b = jnp.where(z1 == zs, pair, 2 * z1 + y)
                d_key, d_value = tile(0, kv[z1, 0], kv[z1, 1], b, False)
                part[z1, 0] = d_key
                part[z1, 1] = d_value
        return 0

    lax.fori_loop(0, zs + 1, own_step, 0)
    dq_own[...] = jnp.transpose(dqt[0])

    def ship(z1, d_key, d_value):
        for r in range(np):
            fsend[z1, r, 0] = d_key[r * half:(r + 1) * half].astype(BF16)
            fsend[z1, r, 1] = d_value[r * half:(r + 1) * half].astype(BF16)

    @pl.when((z == 0) & (y == 1))
    def _():
        ship(zs, part[zs, 0], part[zs, 1])
        for r in range(np):
            pair_fin(r).start()

    @pl.when(z == 0)
    def _():
        dq_recv[...] = jnp.zeros_like(dq_recv)

    def later(r):
        def step(z1, _):
            @pl.when(z1 < z)
            def _():
                fin_copy(r, z1).start()
            return 0
        lax.fori_loop(0, zs, step, 0)

    @pl.when(swapping)
    def _():
        dqt[1] = jnp.zeros_like(dqt[1])
        with jax.named_scope("wait_swap"):
            swap_qd.wait_recv()
            swap_stats.wait_recv()
        stack(1, pair_qd)

        def pair_step(z1, _):
            @pl.when(z1 < z)
            def _():
                with jax.named_scope("pair_tile"):
                    d_key, d_value = tile(1, kv[z1, 0], kv[z1, 1], 2 * z1 + y, False)
                    ship(z1, part[z1, 0] + d_key, part[z1, 1] + d_value)
                fin_copy(0, z1).start()
            return 0

        lax.fori_loop(0, zs, pair_step, 0)

        @pl.when(y == 0)
        def _():
            with jax.named_scope("pair_own"):
                d_key, d_value = tile(1, own[0], own[1], me, False)
                acc[0] += d_key
                acc[1] += d_value

        pair_dq = jnp.transpose(dqt[1]).astype(BF16)
        for r in range(np):
            for g in range(group):
                dq_send[r, g] = pair_dq[g * cap + r * half:g * cap + (r + 1) * half]
            swap_dq(r).start()
        later(1)

    w_copies[0].wait()
    pltpu.make_async_copy(wkv, wkv, w_sem.at[1]).wait()
    width = hold.shape[2] * nb // ns

    def whole(owner, s, n, rows):
        cols = pl.ds(pl.multiple_of((owner * ns + s) * width, width), n * width)
        return dot(gq[rows, :], wq[cols, :], NT) + dot(gkv[rows, :], wkv[cols, :], NT)

    def chip_copy(b):
        return remote(csend.at[b], crcv.at[b], c_send.at[0], c_recv.at[b], heads=other)

    def near_copy(dx, r, i):
        at = (dx - 1, r, pl.ds(*plan[r][i]))
        return remote(
            tsend.at[at], trcv.at[at], t_send.at[0], t_recv.at[dx - 1, first[r] + i], heads=other
        )

    def cross_copy(dx, r, i):
        at = (dx - 1, r, pl.ds(*plan[r][i]))
        return remote(
            xsend.at[at], xrcv.at[at], x_send.at[0], x_recv.at[dx - 1, first[r] + i], heads=across[dx]
        )

    for r in range(np):
        rows = slice(r * half, (r + 1) * half)

        def collect(i, _):
            z2 = zs - i

            @pl.when(((z2 > z) & (z2 < zs)) | ((z2 == zs) & (z == 0) & (y == 0)))
            def _():
                fin_wait(r, z2)
                acc[:, rows, :] += frcv[z2, r].astype(F32)
            return 0

        with jax.named_scope("wait_dq"):
            @pl.when(swapping)
            def _():
                swap_dq(r).wait_recv()
        if r == 0:
            for rr in range(2, np):
                later(rr)
        for g in range(group):
            total = dq_own[g * cap + r * half:g * cap + (r + 1) * half, :] + dq_recv[r, g].astype(F32)
            gq[rows, g * dim:(g + 1) * dim] = (total * scale).astype(BF16)
        with jax.named_scope("collect"):
            lax.fori_loop(0, zs + 1, collect, 0)
        key_total = acc[0, rows, :] * scale
        value_total = acc[1, rows, :]
        dk_ref[rows, :] = key_total
        dv_ref[rows, :] = value_total
        gkv[rows, 0:dim] = key_total.astype(BF16)
        gkv[rows, dim:2 * dim] = value_total.astype(BF16)
        for dx in range(1, nx):
            with jax.named_scope("near"):
                for i, (s, n) in enumerate(plan[r]):
                    terms = whole(across[dx] + 1 - 2 * core, s, n, rows).astype(BF16)
                    for j in range(n):
                        tsend[dx - 1, r, s + j] = terms[:, j * width:(j + 1) * width]
                    near_copy(dx, r, i).start()
            with jax.named_scope("cross"):
                for i, (s, n) in enumerate(plan[r]):
                    terms = whole(across[dx], s, n, rows)
                    for j in range(n):
                        keep[s + j] = terms[:, j * width:(j + 1) * width]
                    near_copy(dx, r, i).wait_recv()
                    for j in range(s, s + n):
                        xsend[dx - 1, r, j] = (keep[j] + trcv[dx - 1, r, j].astype(F32)).astype(BF16)
                    cross_copy(dx, r, i).start()
    everything = slice(0, cap)
    per = ns // nb
    with jax.named_scope("chip_proj"):
        for b in range(nb):
            csend[b] = whole(other, b * per, per, everything).astype(BF16)
            chip_copy(b).start()
        for b in range(nb):
            hold[b] = whole(h, b * per, per, everything)
    with jax.named_scope("chip_wait"):
        for b in range(nb):
            chip_copy(b).wait_recv()
            hold[b] += crcv[b].astype(F32)
    for r in range(np):
        rows = slice(r * half, (r + 1) * half)
        for i, (s, n) in enumerate(plan[r]):
            for dx in range(1, nx):
                with jax.named_scope("wait_cross"):
                    cross_copy(dx, r, i).wait_recv()
            for j in range(s, s + n):
                total = hold[j // per, rows, (j % per) * width:(j % per + 1) * width]
                for dx in range(1, nx):
                    total = total + xrcv[dx - 1, r, j].astype(F32)
                out_ref[rows, j * width:(j + 1) * width] = total.astype(BF16)

    with jax.named_scope("drain"):
        @pl.when(swapping)
        def _():
            swap_qd.wait_send()
            swap_stats.wait_send()
            remote(dq_send, dq_recv, swap_send.at[2], swap_recv.at[2], ctx=pair).wait_send()

        def fins_sent(z1):
            remote(fsend.at[z1], frcv.at[z1], f_send.at[z1], f_recv.at[z1, 0], ctx=pair).wait_send()

        def drain(z2, _):
            @pl.when(z2 > z)
            def _():
                own_copy(z2).wait_send()

            @pl.when(z2 < z)
            def _():
                fins_sent(z2)
            return 0

        lax.fori_loop(0, zs, drain, 0)

        @pl.when((z == 0) & (y == 0))
        def _():
            pair_own_copy.wait_send()

        @pl.when((z == 0) & (y == 1))
        def _():
            fins_sent(zs)

        remote(csend, crcv, c_send.at[0], c_recv.at[0], heads=other).wait_send()
        remote(tsend, trcv, t_send.at[0], t_recv.at[0, 0], heads=other).wait_send()
        for dx in range(1, nx):
            remote(
                xsend.at[dx - 1], xrcv.at[dx - 1], x_send.at[0], x_recv.at[dx - 1, 0], heads=across[dx]
            ).wait_send()


def emit(a, b, c, a_hbm, b_hbm, c_hbm, sem):
    copies = [
        pltpu.make_async_copy(src, dst, sem.at[i])
        for i, (src, dst) in enumerate(((a, a_hbm), (b, b_hbm), (c, c_hbm)))
    ]
    for copy in copies:
        copy.start()
    for copy in copies:
        copy.wait()


def on_device(
    n, nh, queries, key_states, value_states, attention_out, out_grad, log_sum_exp, block_counts,
    w_query, w_key, w_value,
):
    zs, nx, ns, nb = n // 2, nh // 2, 4, 2
    cap, dim = key_states.shape
    width = queries.shape[1]
    rows = width // dim * cap
    model = w_query.shape[0]
    mine = model // nh
    chunk = mine // ns
    vmem = pl.BlockSpec(memory_space=pltpu.VMEM)
    half = BLOCK
    np = cap // half
    blocks = sum(len(p) for p in row_blocks(np, ns))
    hbm = pl.BlockSpec(memory_space=pltpu.HBM)
    dma = pltpu.SemaphoreType.DMA
    results = pl.pallas_call(
        functools.partial(kernel, zs, nx, ns, nb),
        out_shape=(
            jax.ShapeDtypeStruct((cap, mine), BF16),
            jax.ShapeDtypeStruct((cap, dim), F32),
            jax.ShapeDtypeStruct((cap, dim), F32),
        ),
        in_specs=[hbm] * 10,
        out_specs=(vmem, vmem, vmem),
        scratch_shapes=[
            pltpu.SMEM(block_counts.shape, jnp.int32),
            pltpu.VMEM((2, cap, dim), BF16),
            pltpu.VMEM((2, cap, width), BF16),
            pltpu.VMEM((cap, width), BF16),
            pltpu.VMEM(log_sum_exp.shape, F32),
            pltpu.VMEM((2, cap, width), BF16),
            pltpu.VMEM((model, width), BF16),
            pltpu.VMEM((model, 2 * dim), BF16),
            pltpu.VMEM((2, rows, dim), BF16),
            pltpu.VMEM((2, rows, dim), BF16),
            pltpu.VMEM((2, 2, rows), F32),
            pltpu.VMEM((2, dim, rows), F32),
            pltpu.VMEM((rows, dim), F32),
            pltpu.VMEM((np, width // dim, half, dim), BF16),
            pltpu.VMEM((np, width // dim, half, dim), BF16),
            pltpu.VMEM((cap, width), BF16),
            pltpu.VMEM((cap, 2 * dim), BF16),
            pltpu.VMEM((2, cap, dim), F32),
            pltpu.VMEM((zs + 1, 2, cap, dim), BF16),
            pltpu.VMEM((zs + 1, 2, cap, dim), F32),
            pltpu.VMEM((zs + 1, np, 2, half, dim), BF16),
            pltpu.VMEM((zs + 1, np, 2, half, dim), BF16),
            pltpu.VMEM((ns, half, chunk), F32),
            pltpu.VMEM((nb, cap, mine // nb), F32),
            pltpu.VMEM((nb, cap, mine // nb), BF16),
            pltpu.VMEM((nb, cap, mine // nb), BF16),
            pltpu.VMEM((nx - 1, np, ns, half, chunk), BF16),
            pltpu.VMEM((nx - 1, np, ns, half, chunk), BF16),
            pltpu.VMEM((nx - 1, np, ns, half, chunk), BF16),
            pltpu.VMEM((nx - 1, np, ns, half, chunk), BF16),
            dma((5,)),
            dma((2,)),
            dma((zs + 1,)),
            dma((zs + 1,)),
            dma((3,)),
            dma((2 + np,)),
            dma((zs + 1,)),
            dma((zs + 1, np)),
            dma((1,)),
            dma((nb,)),
            dma((1,)),
            dma((nx - 1, blocks)),
            dma((1,)),
            dma((nx - 1, blocks)),
        ],
        compiler_params=pltpu.CompilerParams(
            collective_id=0, has_side_effects=True, vmem_limit_bytes=52 * 1024 * 1024
        ),
    )(
        *(
            pltpu.with_memory_space_constraint(a, pltpu.HBM)
            for a in (
                queries, key_states, value_states, attention_out, out_grad, log_sum_exp,
                block_counts, w_query, w_key, w_value,
            )
        )
    )
    return pl.pallas_call(
        emit,
        out_shape=tuple(jax.ShapeDtypeStruct(a.shape, a.dtype) for a in results),
        in_specs=[vmem] * 3,
        out_specs=(hbm,) * 3,
        scratch_shapes=[dma((3,))],
    )(*(pltpu.with_memory_space_constraint(a, pltpu.VMEM) for a in results))


def solution(mesh):
    return jax.shard_map(
        functools.partial(on_device, mesh.shape["ctx"], mesh.shape["heads"]),
        mesh=mesh,
        in_specs=(
            P("ctx", "heads"),
            P("ctx", "heads"),
            P("ctx", "heads"),
            P("ctx", "heads"),
            P("ctx", "heads"),
            P("heads", "ctx"),
            P(),
            P(None, "heads"),
            P(None, "heads"),
            P(None, "heads"),
        ),
        out_specs=(P("ctx", "heads"), P("ctx", "heads"), P("ctx", "heads")),
        check_vma=False,
    )
```

time: 38.5 us -> 35.8 us (0.930)
  local copies, waits for them, and re-layouts: 2.03 us -> 0 us
  Pallas kernels: 35.7 us -> 35 us
    unnamed x3 -> x0, local copies, waits for them, and re-layouts: 2.03 us -> none
    pallas_call x1 -> x2, Pallas kernels: 35.7 us -> 35 us  [the longest x1 34.2 us: on_device(): pl.pallas_call(functools.partial(kernel, zs, nx, ns, nb), out_shape=(jax....]
where the time goes in v1:
time: 35.8 us; the launch traced here: 35.6 us
  Pallas kernels  35 us (98%)
  between operations  0.64 us (2%)
    pallas_call x1, Pallas kernels, on_device(): pl.pallas_call(functools.partial(kernel, zs, nx, ns, nb), out_shape=(jax....  34.2 us
    pallas_call x1, Pallas kernels, on_device(): pl.pallas_call(emit, out_shape=tuple((jax.ShapeDtypeStruct(a.shape, a.dty...  0.83 us

profile of v1, /device:TPU:0, one launch (start us, length us, event | category | flops | bytes accessed | tf_op | source)
XLA Modules:
  0.0 35.6 jit_solution(3569548956855799590)
XLA Ops:
  0.6 34.2 %shard_map.121 = (bf16[192,1024]{1,0:T(8,128)(2,1)S(1)}, f32[192,128]{1,0:T(8,128)S(1)}, f32[192,128]{1,0:T(8,128)S(1)}) custom-call(bf16[192,512]{1,0:T(8,128)(2,1)} %q_hbm.1, bf16[192,128]{1,0:T(8,128)(2,1)} %k_hbm.1, bf16[192,128]{1,0:T(8,128)(2,1)} %v_hbm.1, bf16[192,512]{1,0:T(8,128)(2,1)} %o_hbm.1, bf16[192,512]{1,0:T(8,128)(2,1)} %do_hbm.1, ...), custom_call_target="tpu_custom_call" | custom-call | tf_op jit(solution)/shard_map/pallas_call | solution.py:441
  34.8 0.8 %shard_map.122 = (bf16[192,1024]{1,0:T(8,128)(2,1)}, f32[192,128]{1,0:T(8,128)}, f32[192,128]{1,0:T(8,128)}) custom-call(bf16[192,1024]{1,0:T(8,128)(2,1)S(1)} %get-tuple-element.6.a, f32[192,128]{1,0:T(8,128)S(1)} %get-tuple-element.7.b, f32[192,128]{1,0:T(8,128)S(1)} %get-tuple-element.8.c), custom_call_target="tpu_custom_call" | custom-call | tf_op jit(solution)/shard_map/pallas_call | solution.py:508

commit v2 on v1

--- a/solution.py
+++ b/solution.py
@@ -33,13 +33,13 @@
 
 
 def kernel(
-    zs, nx, ns, nb,
+    zs, nx, ns,
     q_hbm, k_hbm, v_hbm, o_hbm, do_hbm, lse_hbm, cnt_hbm, wq_hbm, wk_hbm, wv_hbm,
     out_ref, dk_ref, dv_ref,
-    cnt_ref, own, qd, o_ref, lse_ref, pair_qd, wq, wkv, qs, dos, stats, dqt,
-    dq_own, dq_send, dq_recv, gq, gkv, acc, kv, part, fsend, frcv, keep, hold, csend, crcv, tsend, trcv, xsend, xrcv,
-    in_sem, w_sem, own_send, kv_recv, swap_send, swap_recv, f_send, f_recv,
-    c_send, c_recv, t_send, t_recv, x_send, x_recv,
+    cnt_ref, own, qd, o_ref, lse_ref, pair_qd, w, qs, dos, stats, dqt,
+    dq_own, dq_send, dq_recv, gs, acc, kv, part, fsend, frcv, hold, xsend, xrcv,
+    in_sem, w_sem, w_send, w_recv, own_send, kv_recv, swap_send, swap_recv, f_send, f_recv,
+    g_send, g_recv, x_send, x_recv, turn,
 ):
     cap, dim = own.shape[1:]
     group = qd.shape[2] // dim
@@ -67,18 +67,34 @@
     ]
     for copy in loads:
         copy.start()
-    w_copies = [
-        pltpu.make_async_copy(wq_hbm, wq, w_sem.at[0]),
-        pltpu.make_async_copy(wk_hbm, wkv.at[:, pl.ds(0, dim)], w_sem.at[1]),
-        pltpu.make_async_copy(wv_hbm, wkv.at[:, pl.ds(dim, dim)], w_sem.at[1]),
-    ]
-
     def remote(src, dst, send, recv, **device):
         return pltpu.make_async_remote_copy(
             src_ref=src, dst_ref=dst, send_sem=send, recv_sem=recv,
             device_id=device, device_id_type=pl.DeviceIdType.MESH,
         )
 
+    mine = w.shape[1] // nx
+    wide = qd.shape[2]
+    weights = ((wq_hbm, 0, wide), (wk_hbm, wide, dim), (wv_hbm, wide + dim, dim))
+
+    def w_rows(owner, src):
+        return src.at[pl.ds(pl.multiple_of(owner * mine, mine), mine), :]
+
+    w_loads = [
+        pltpu.make_async_copy(
+            w_rows(across[dx], src), w.at[0, pl.ds(dx * mine, mine), pl.ds(at, size)], w_sem.at[0]
+        )
+        for dx in range(nx)
+        for src, at, size in weights
+    ]
+    w_shares = [
+        remote(
+            w_rows(across[dx] + 1 - 2 * core, src), w.at[1, pl.ds(dx * mine, mine), pl.ds(at, size)],
+            w_send.at[0], w_recv.at[0], heads=other,
+        )
+        for dx in range(nx)
+        for src, at, size in weights
+    ]
     barrier = pltpu.get_barrier_semaphore()
 
     def greet(**device):
@@ -101,7 +117,7 @@
     pltpu.make_async_copy(qd, qd, in_sem.at[1]).wait()
     for copy in loads[4:]:
         copy.wait()
-    for copy in w_copies:
+    for copy in w_loads:
         copy.start()
     with jax.named_scope("barrier"):
         pl.semaphore_wait(barrier, zs + nx)
@@ -114,7 +130,10 @@
     def arrived(z1):
         remote(kv.at[z1], kv.at[z1], own_send.at[z1], kv_recv.at[z1], ctx=pair).wait_recv()
 
-    swap_qd = remote(qd, pair_qd, swap_send.at[0], swap_recv.at[0], ctx=pair)
+    swap_q, swap_do = (
+        remote(qd.at[i], pair_qd.at[i], swap_send.at[3 * i], swap_recv.at[(2 + np) * i], ctx=pair)
+        for i in range(2)
+    )
     swap_stats = remote(stats.at[0], stats.at[1], swap_send.at[1], swap_recv.at[1], ctx=pair)
 
     def swap_dq(r):
@@ -136,10 +155,13 @@
         ).wait_recv()
 
     swapping = z > 0
-
-    @pl.when(swapping)
-    def _():
-        swap_qd.start()
+    early = swapping & (core == 0)
+    late = swapping & (core == 1)
+
+    @pl.when(early)
+    def _():
+        swap_q.start()
+        swap_do.start()
 
     @pl.when((z == 0) & (y == 0))
     def _():
@@ -208,6 +230,53 @@
         acc[0] = d_key
         acc[1] = d_value
 
+    for copy in w_shares:
+        copy.start()
+
+    @pl.when(early)
+    def _():
+        with jax.named_scope("hand_over"):
+            swap_q.wait_send()
+            pl.semaphore_signal(
+                turn, inc=1, device_id={"heads": other}, device_id_type=pl.DeviceIdType.MESH
+            )
+
+    @pl.when(late)
+    def _():
+        with jax.named_scope("my_turn"):
+            pl.semaphore_wait(turn, 1)
+            swap_q.start()
+            swap_do.start()
+
+    def ship(z1, d_key, d_value):
+        for r in range(np):
+            fsend[z1, r, 0] = d_key[r * half:(r + 1) * half].astype(BF16)
+            fsend[z1, r, 1] = d_value[r * half:(r + 1) * half].astype(BF16)
+
+    def later(r):
+        def step(z1, _):
+            @pl.when(z1 < z)
+            def _():
+                fin_copy(r, z1).start()
+            return 0
+        lax.fori_loop(0, zs, step, 0)
+
+    def swapped():
+        dqt[1] = jnp.zeros_like(dqt[1])
+        with jax.named_scope("wait_swap"):
+            swap_q.wait_recv()
+            swap_do.wait_recv()
+            swap_stats.wait_recv()
+        stack(1, pair_qd)
+
+    def pair_tile(z1):
+        with jax.named_scope("pair_tile"):
+            d_key, d_value = tile(1, kv[z1, 0], kv[z1, 1], 2 * z1 + y, False)
+            ship(z1, part[z1, 0] + d_key, part[z1, 1] + d_value)
+        fin_copy(0, z1).start()
+
+    pl.when(early)(swapped)
+
     def own_step(z1, _):
         @pl.when((z1 < z) | ((z1 == zs) & (z == 0) & (y == 1)))
         def _():
@@ -218,15 +287,18 @@
                 d_key, d_value = tile(0, kv[z1, 0], kv[z1, 1], b, False)
                 part[z1, 0] = d_key
                 part[z1, 1] = d_value
+
+        @pl.when((z1 < z) & early)
+        def _():
+            pair_tile(z1)
         return 0
 
     lax.fori_loop(0, zs + 1, own_step, 0)
-    dq_own[...] = jnp.transpose(dqt[0])
-
-    def ship(z1, d_key, d_value):
-        for r in range(np):
-            fsend[z1, r, 0] = d_key[r * half:(r + 1) * half].astype(BF16)
-            fsend[z1, r, 1] = d_value[r * half:(r + 1) * half].astype(BF16)
+
+    @pl.when(early)
+    def _():
+        for r in range(1, np):
+            later(r)
 
     @pl.when((z == 0) & (y == 1))
     def _():
@@ -238,33 +310,24 @@
     def _():
         dq_recv[...] = jnp.zeros_like(dq_recv)
 
-    def later(r):
-        def step(z1, _):
-            @pl.when(z1 < z)
-            def _():
-                fin_copy(r, z1).start()
-            return 0
-        lax.fori_loop(0, zs, step, 0)
-
-    @pl.when(swapping)
-    def _():
-        dqt[1] = jnp.zeros_like(dqt[1])
-        with jax.named_scope("wait_swap"):
-            swap_qd.wait_recv()
-            swap_stats.wait_recv()
-        stack(1, pair_qd)
+    dq_own[...] = jnp.transpose(dqt[0])
+
+    @pl.when(late)
+    def _():
+        swapped()
 
         def pair_step(z1, _):
             @pl.when(z1 < z)
             def _():
-                with jax.named_scope("pair_tile"):
-                    d_key, d_value = tile(1, kv[z1, 0], kv[z1, 1], 2 * z1 + y, False)
-                    ship(z1, part[z1, 0] + d_key, part[z1, 1] + d_value)
-                fin_copy(0, z1).start()
+                pair_tile(z1)
             return 0
 
         lax.fori_loop(0, zs, pair_step, 0)
-
+        for r in range(1, np):
+            later(r)
+
+    @pl.when(swapping)
+    def _():
         @pl.when(y == 0)
         def _():
             with jax.named_scope("pair_own"):
@@ -277,24 +340,17 @@
             for g in range(group):
                 dq_send[r, g] = pair_dq[g * cap + r * half:g * cap + (r + 1) * half]
             swap_dq(r).start()
-        later(1)
-
-    w_copies[0].wait()
-    pltpu.make_async_copy(wkv, wkv, w_sem.at[1]).wait()
-    width = hold.shape[2] * nb // ns
-
-    def whole(owner, s, n, rows):
-        cols = pl.ds(pl.multiple_of((owner * ns + s) * width, width), n * width)
-        return dot(gq[rows, :], wq[cols, :], NT) + dot(gkv[rows, :], wkv[cols, :], NT)
-
-    def chip_copy(b):
-        return remote(csend.at[b], crcv.at[b], c_send.at[0], c_recv.at[b], heads=other)
-
-    def near_copy(dx, r, i):
-        at = (dx - 1, r, pl.ds(*plan[r][i]))
-        return remote(
-            tsend.at[at], trcv.at[at], t_send.at[0], t_recv.at[dx - 1, first[r] + i], heads=other
-        )
+
+    pltpu.make_async_copy(w.at[0], w.at[0], w_sem.at[0]).wait()
+    remote(w.at[1], w.at[1], w_send.at[0], w_recv.at[0], heads=other).wait_recv()
+    width = mine // ns
+
+    def g_copy(r):
+        return remote(gs.at[0, r], gs.at[1, r], g_send.at[0], g_recv.at[r], heads=other)
+
+    def whole(dx, s, n, r):
+        cols = slice(dx * mine + s * width, dx * mine + (s + n) * width)
+        return dot(gs[0, r], w[0, cols, :], NT) + dot(gs[1, r], w[1, cols, :], NT)
 
     def cross_copy(dx, r, i):
         at = (dx - 1, r, pl.ds(*plan[r][i]))
@@ -318,48 +374,31 @@
             @pl.when(swapping)
             def _():
                 swap_dq(r).wait_recv()
-        if r == 0:
-            for rr in range(2, np):
-                later(rr)
         for g in range(group):
             total = dq_own[g * cap + r * half:g * cap + (r + 1) * half, :] + dq_recv[r, g].astype(F32)
-            gq[rows, g * dim:(g + 1) * dim] = (total * scale).astype(BF16)
+            gs[0, r, :, g * dim:(g + 1) * dim] = (total * scale).astype(BF16)
         with jax.named_scope("collect"):
             lax.fori_loop(0, zs + 1, collect, 0)
         key_total = acc[0, rows, :] * scale
         value_total = acc[1, rows, :]
         dk_ref[rows, :] = key_total
         dv_ref[rows, :] = value_total
-        gkv[rows, 0:dim] = key_total.astype(BF16)
-        gkv[rows, dim:2 * dim] = value_total.astype(BF16)
-        for dx in range(1, nx):
-            with jax.named_scope("near"):
+        gs[0, r, :, wide:wide + dim] = key_total.astype(BF16)
+        gs[0, r, :, wide + dim:wide + 2 * dim] = value_total.astype(BF16)
+        g_copy(r).start()
+        with jax.named_scope("wait_g"):
+            g_copy(r).wait_recv()
+        with jax.named_scope("project"):
+            for dx in range(1, nx):
                 for i, (s, n) in enumerate(plan[r]):
-                    terms = whole(across[dx] + 1 - 2 * core, s, n, rows).astype(BF16)
+                    terms = whole(dx, s, n, r).astype(BF16)
                     for j in range(n):
-                        tsend[dx - 1, r, s + j] = terms[:, j * width:(j + 1) * width]
-                    near_copy(dx, r, i).start()
-            with jax.named_scope("cross"):
-                for i, (s, n) in enumerate(plan[r]):
-                    terms = whole(across[dx], s, n, rows)
-                    for j in range(n):
-                        keep[s + j] = terms[:, j * width:(j + 1) * width]
-                    near_copy(dx, r, i).wait_recv()
-                    for j in range(s, s + n):
-                        xsend[dx - 1, r, j] = (keep[j] + trcv[dx - 1, r, j].astype(F32)).astype(BF16)
+                        xsend[dx - 1, r, s + j] = terms[:, j * width:(j + 1) * width]
                     cross_copy(dx, r, i).start()
-    everything = slice(0, cap)
-    per = ns // nb
-    with jax.named_scope("chip_proj"):
-        for b in range(nb):
-            csend[b] = whole(other, b * per, per, everything).astype(BF16)
-            chip_copy(b).start()
-        for b in range(nb):
-            hold[b] = whole(h, b * per, per, everything)
-    with jax.named_scope("chip_wait"):
-        for b in range(nb):
-            chip_copy(b).wait_recv()
-            hold[b] += crcv[b].astype(F32)
+    with jax.named_scope("own_proj"):
+        for r in range(np):
+            for s in range(0, ns, 2):
+                hold[r * half:(r + 1) * half, s * width:(s + 2) * width] = whole(0, s, 2, r)
     for r in range(np):
         rows = slice(r * half, (r + 1) * half)
         for i, (s, n) in enumerate(plan[r]):
@@ -367,15 +406,18 @@
                 with jax.named_scope("wait_cross"):
                     cross_copy(dx, r, i).wait_recv()
             for j in range(s, s + n):
-                total = hold[j // per, rows, (j % per) * width:(j % per + 1) * width]
+                cols = slice(j * width, (j + 1) * width)
+                total = hold[rows, cols]
                 for dx in range(1, nx):
                     total = total + xrcv[dx - 1, r, j].astype(F32)
-                out_ref[rows, j * width:(j + 1) * width] = total.astype(BF16)
+                out_ref[rows, cols] = total.astype(BF16)
 
     with jax.named_scope("drain"):
+        pl.when(late)(swap_q.wait_send)
+
         @pl.when(swapping)
         def _():
-            swap_qd.wait_send()
+            swap_do.wait_send()
             swap_stats.wait_send()
             remote(dq_send, dq_recv, swap_send.at[2], swap_recv.at[2], ctx=pair).wait_send()
 
@@ -402,8 +444,8 @@
         def _():
             fins_sent(zs)
 
-        remote(csend, crcv, c_send.at[0], c_recv.at[0], heads=other).wait_send()
-        remote(tsend, trcv, t_send.at[0], t_recv.at[0, 0], heads=other).wait_send()
+        remote(w.at[1], w.at[1], w_send.at[0], w_recv.at[0], heads=other).wait_send()
+        remote(gs.at[0], gs.at[1], g_send.at[0], g_recv.at[0], heads=other).wait_send()
         for dx in range(1, nx):
             remote(
                 xsend.at[dx - 1], xrcv.at[dx - 1], x_send.at[0], x_recv.at[dx - 1, 0], heads=across[dx]
@@ -425,7 +467,7 @@
     n, nh, queries, key_states, value_states, attention_out, out_grad, log_sum_exp, block_counts,
     w_query, w_key, w_value,
 ):
-    zs, nx, ns, nb = n // 2, nh // 2, 4, 2
+    zs, nx, ns = n // 2, nh // 2, 4
     cap, dim = key_states.shape
     width = queries.shape[1]
     rows = width // dim * cap
@@ -439,7 +481,7 @@
     hbm = pl.BlockSpec(memory_space=pltpu.HBM)
     dma = pltpu.SemaphoreType.DMA
     results = pl.pallas_call(
-        functools.partial(kernel, zs, nx, ns, nb),
+        functools.partial(kernel, zs, nx, ns),
         out_shape=(
             jax.ShapeDtypeStruct((cap, mine), BF16),
             jax.ShapeDtypeStruct((cap, dim), F32),
@@ -454,8 +496,7 @@
             pltpu.VMEM((cap, width), BF16),
             pltpu.VMEM(log_sum_exp.shape, F32),
             pltpu.VMEM((2, cap, width), BF16),
-            pltpu.VMEM((model, width), BF16),
-            pltpu.VMEM((model, 2 * dim), BF16),
+            pltpu.VMEM((2, nx * mine, width + 2 * dim), BF16),
             pltpu.VMEM((2, rows, dim), BF16),
             pltpu.VMEM((2, rows, dim), BF16),
             pltpu.VMEM((2, 2, rows), F32),
@@ -463,35 +504,30 @@
             pltpu.VMEM((rows, dim), F32),
             pltpu.VMEM((np, width // dim, half, dim), BF16),
             pltpu.VMEM((np, width // dim, half, dim), BF16),
-            pltpu.VMEM((cap, width), BF16),
-            pltpu.VMEM((cap, 2 * dim), BF16),
+            pltpu.VMEM((2, np, half, width + 2 * dim), BF16),
             pltpu.VMEM((2, cap, dim), F32),
             pltpu.VMEM((zs + 1, 2, cap, dim), BF16),
             pltpu.VMEM((zs + 1, 2, cap, dim), F32),
             pltpu.VMEM((zs + 1, np, 2, half, dim), BF16),
             pltpu.VMEM((zs + 1, np, 2, half, dim), BF16),
-            pltpu.VMEM((ns, half, chunk), F32),
-            pltpu.VMEM((nb, cap, mine // nb), F32),
-            pltpu.VMEM((nb, cap, mine // nb), BF16),
-            pltpu.VMEM((nb, cap, mine // nb), BF16),
-            pltpu.VMEM((nx - 1, np, ns, half, chunk), BF16),
-            pltpu.VMEM((nx - 1, np, ns, half, chunk), BF16),
+            pltpu.VMEM((cap, mine), F32),
             pltpu.VMEM((nx - 1, np, ns, half, chunk), BF16),
             pltpu.VMEM((nx - 1, np, ns, half, chunk), BF16),
             dma((5,)),
-            dma((2,)),
+            dma((1,)),
+            dma((1,)),
+            dma((1,)),
             dma((zs + 1,)),
             dma((zs + 1,)),
-            dma((3,)),
-            dma((2 + np,)),
+            dma((4,)),
+            dma((3 + np,)),
             dma((zs + 1,)),
             dma((zs + 1, np)),
             dma((1,)),
-            dma((nb,)),
+            dma((np,)),
             dma((1,)),
             dma((nx - 1, blocks)),
-            dma((1,)),
-            dma((nx - 1, blocks)),
+            pltpu.SemaphoreType.REGULAR,
         ],
         compiler_params=pltpu.CompilerParams(
             collective_id=0, has_side_effects=True, vmem_limit_bytes=52 * 1024 * 1024

time: 35.8 us -> 34.6 us (0.966)
  Pallas kernels: 35 us -> 33.8 us
    pallas_call x1, Pallas kernels: 34.2 us -> 33 us  [on_device(): pl.pallas_call(functools.partial(kernel, zs, nx, ns), out_shape=(jax.Shap...]
where the time goes in v2:
time: 34.6 us; the launch traced here: 34.5 us
  Pallas kernels  33.8 us (98%)
  between operations  0.64 us (2%)
    pallas_call x1, Pallas kernels, on_device(): pl.pallas_call(functools.partial(kernel, zs, nx, ns), out_shape=(jax.Shap...  33 us
    pallas_call x1, Pallas kernels, on_device(): pl.pallas_call(emit, out_shape=tuple((jax.ShapeDtypeStruct(a.shape, a.dty...  0.83 us

profile of v2, /device:TPU:0, one launch (start us, length us, event | category | flops | bytes accessed | tf_op | source)
XLA Modules:
  0.0 34.5 jit_solution(16931228996413099746)
XLA Ops:
  0.6 33.0 %shard_map.121 = (bf16[192,1024]{1,0:T(8,128)(2,1)S(1)}, f32[192,128]{1,0:T(8,128)S(1)}, f32[192,128]{1,0:T(8,128)S(1)}) custom-call(bf16[192,512]{1,0:T(8,128)(2,1)} %q_hbm.1, bf16[192,128]{1,0:T(8,128)(2,1)} %k_hbm.1, bf16[192,128]{1,0:T(8,128)(2,1)} %v_hbm.1, bf16[192,512]{1,0:T(8,128)(2,1)} %o_hbm.1, bf16[192,512]{1,0:T(8,128)(2,1)} %do_hbm.1, ...), custom_call_target="tpu_custom_call" | custom-call | tf_op jit(solution)/shard_map/pallas_call | solution.py:483
  33.7 0.8 %shard_map.122 = (bf16[192,1024]{1,0:T(8,128)(2,1)}, f32[192,128]{1,0:T(8,128)}, f32[192,128]{1,0:T(8,128)}) custom-call(bf16[192,1024]{1,0:T(8,128)(2,1)S(1)} %get-tuple-element.6.a, f32[192,128]{1,0:T(8,128)S(1)} %get-tuple-element.7.b, f32[192,128]{1,0:T(8,128)S(1)} %get-tuple-element.8.c), custom_call_target="tpu_custom_call" | custom-call | tf_op jit(solution)/shard_map/pallas_call | solution.py:544

commit v3 on v2

--- a/solution.py
+++ b/solution.py
@@ -9,6 +9,7 @@
 from jax.sharding import PartitionSpec as P
 
 BLOCK = 64
+EMIT = 4
 LOG2E = math.log2(math.e)
 F32 = jnp.float32
 BF16 = jnp.bfloat16
@@ -36,13 +37,13 @@
     zs, nx, ns,
     q_hbm, k_hbm, v_hbm, o_hbm, do_hbm, lse_hbm, cnt_hbm, wq_hbm, wk_hbm, wv_hbm,
     out_ref, dk_ref, dv_ref,
-    cnt_ref, own, qd, o_ref, lse_ref, pair_qd, w, qs, dos, stats, dqt,
-    dq_own, dq_send, dq_recv, gs, acc, kv, part, fsend, frcv, hold, xsend, xrcv,
+    cnt_ref, own, qd, o_ref, lse_ref, w, stats, dqt,
+    dq_own, dq_send, dq_recv, gs, acc, kv, part, fsend, frcv, keep, hold, xsend, xrcv,
     in_sem, w_sem, w_send, w_recv, own_send, kv_recv, swap_send, swap_recv, f_send, f_recv,
     g_send, g_recv, x_send, x_recv, turn,
 ):
     cap, dim = own.shape[1:]
-    group = qd.shape[2] // dim
+    group = qd.shape[1]
     np = dq_send.shape[0]
     half = cap // np
     scale = 1.0 / math.sqrt(dim)
@@ -58,15 +59,6 @@
     other = h + 1 - 2 * core
     across = [2 * lax.rem(x + dx, nx) + core for dx in range(nx)]
 
-    loads = [
-        pltpu.make_async_copy(src, dst, in_sem.at[i])
-        for src, dst, i in (
-            (k_hbm, own.at[0], 0), (v_hbm, own.at[1], 0), (q_hbm, qd.at[0], 1), (do_hbm, qd.at[1], 1),
-            (o_hbm, o_ref, 2), (lse_hbm, lse_ref, 3), (cnt_hbm, cnt_ref, 4),
-        )
-    ]
-    for copy in loads:
-        copy.start()
     def remote(src, dst, send, recv, **device):
         return pltpu.make_async_remote_copy(
             src_ref=src, dst_ref=dst, send_sem=send, recv_sem=recv,
@@ -74,7 +66,7 @@
         )
 
     mine = w.shape[1] // nx
-    wide = qd.shape[2]
+    wide = group * dim
     weights = ((wq_hbm, 0, wide), (wk_hbm, wide, dim), (wv_hbm, wide + dim, dim))
 
     def w_rows(owner, src):
@@ -113,9 +105,24 @@
     greet(heads=other)
     for dx in range(1, nx):
         greet(heads=across[dx])
+
+    heads = [pl.ds(g * dim, dim) for g in range(group)]
+    loads = [
+        pltpu.make_async_copy(src, dst, in_sem.at[i])
+        for src, dst, i in (
+            (k_hbm, own.at[0], 0), (v_hbm, own.at[1], 0),
+            *((q_hbm.at[:, heads[g]], qd.at[0, g, 0], 1) for g in range(group)),
+            *((do_hbm.at[:, heads[g]], qd.at[0, g, 1], 1) for g in range(group)),
+            *((o_hbm.at[:, heads[g]], o_ref.at[g], 2) for g in range(group)),
+            (lse_hbm, lse_ref, 3), (cnt_hbm, cnt_ref, 4),
+        )
+    ]
+    for copy in loads:
+        copy.start()
     pltpu.make_async_copy(own, own, in_sem.at[0]).wait()
-    pltpu.make_async_copy(qd, qd, in_sem.at[1]).wait()
-    for copy in loads[4:]:
+    pltpu.make_async_copy(qd.at[0], qd.at[0], in_sem.at[1]).wait()
+    pltpu.make_async_copy(o_ref, o_ref, in_sem.at[2]).wait()
+    for copy in loads[-2:]:
         copy.wait()
     for copy in w_loads:
         copy.start()
@@ -130,14 +137,18 @@
     def arrived(z1):
         remote(kv.at[z1], kv.at[z1], own_send.at[z1], kv_recv.at[z1], ctx=pair).wait_recv()
 
-    swap_q, swap_do = (
-        remote(qd.at[i], pair_qd.at[i], swap_send.at[3 * i], swap_recv.at[(2 + np) * i], ctx=pair)
-        for i in range(2)
+    swap_qd = [
+        remote(qd.at[0, g], qd.at[1, g], swap_send.at[g], swap_recv.at[g], ctx=pair)
+        for g in range(group)
+    ]
+    swap_stats = remote(
+        stats.at[0], stats.at[1], swap_send.at[group], swap_recv.at[group], ctx=pair
     )
-    swap_stats = remote(stats.at[0], stats.at[1], swap_send.at[1], swap_recv.at[1], ctx=pair)
 
     def swap_dq(r):
-        return remote(dq_send.at[r], dq_recv.at[r], swap_send.at[2], swap_recv.at[2 + r], ctx=pair)
+        return remote(
+            dq_send.at[r], dq_recv.at[r], swap_send.at[group + 1], swap_recv.at[group + 1 + r], ctx=pair
+        )
 
     def fin_copy(r, z1):
         return remote(
@@ -160,8 +171,8 @@
 
     @pl.when(early)
     def _():
-        swap_q.start()
-        swap_do.start()
+        for copy in swap_qd:
+            copy.start()
 
     @pl.when((z == 0) & (y == 0))
     def _():
@@ -180,13 +191,10 @@
     lane = lax.broadcasted_iota(jnp.int32, (1, group * cap), 1)
     row = lax.rem(lane, cap)
     alive = row < cnt_ref[me] * BLOCK
-    prod = jnp.concatenate(
-        [
-            qd[1, :, g * dim:(g + 1) * dim].astype(F32) * o_ref[:, g * dim:(g + 1) * dim].astype(F32)
-            for g in range(group)
-        ],
-        axis=0,
-    )
+    def flat(ref):
+        return ref[...].reshape(group * cap, dim)
+
+    prod = flat(qd.at[0, :, 1]).astype(F32) * flat(o_ref).astype(F32)
     stats[0, 1:2] = lax.dot_general(
         jnp.ones((8, dim), F32), prod, NT,
         preferred_element_type=F32, precision=lax.Precision.HIGHEST,
@@ -194,31 +202,27 @@
     lse_row = jnp.concatenate([lse_ref[g:g + 1, :] for g in range(group)], axis=1)
     stats[0, 0:1] = jnp.where(alive, lse_row * LOG2E, 1e30)
 
-    def stack(who, src):
-        for g in range(group):
-            cols = slice(g * dim, (g + 1) * dim)
-            qs[who, g * cap:(g + 1) * cap, :] = src[0, :, cols]
-            dos[who, g * cap:(g + 1) * cap, :] = src[1, :, cols]
-
-    stack(0, qd)
-
     @pl.when(swapping)
     def _():
         swap_stats.start()
 
     key_row = lax.broadcasted_iota(jnp.int32, (cap, group * cap), 0)
 
+    def products(key, value, query, out_grad, lse, delta, visible):
+        scores = dot(key, query, NT)
+        prob_grad = dot(value, out_grad, NT)
+        prob = jnp.where(visible, jnp.exp2(scores * (scale * LOG2E) - lse), 0.0)
+        grad = (prob * (prob_grad - delta)).astype(BF16)
+        return dot(grad, query), dot(prob.astype(BF16), out_grad), dot(key, grad, TN)
+
     def tile(who, key, value, b, diagonal):
-        scores = dot(key, qs[who], NT)
-        prob_grad = dot(value, dos[who], NT)
         visible = key_row < cnt_ref[b] * BLOCK
         if diagonal:
             visible = visible & (key_row <= row)
-        prob = jnp.where(visible, jnp.exp2(scores * (scale * LOG2E) - stats[who, 0:1]), 0.0)
-        grad = (prob * (prob_grad - stats[who, 1:2])).astype(BF16)
-        d_value = dot(prob.astype(BF16), dos[who])
-        d_key = dot(grad, qs[who])
-        terms = dot(key, grad, TN)
+        d_key, d_value, terms = products(
+            key, value, flat(qd.at[who, :, 0]), flat(qd.at[who, :, 1]),
+            stats[who, 0:1], stats[who, 1:2], visible,
+        )
         if diagonal:
             dqt[who] = terms
         else:
@@ -236,7 +240,8 @@
     @pl.when(early)
     def _():
         with jax.named_scope("hand_over"):
-            swap_q.wait_send()
+            for copy in swap_qd[:group // 2]:
+                copy.wait_send()
             pl.semaphore_signal(
                 turn, inc=1, device_id={"heads": other}, device_id_type=pl.DeviceIdType.MESH
             )
@@ -245,37 +250,48 @@
     def _():
         with jax.named_scope("my_turn"):
             pl.semaphore_wait(turn, 1)
-            swap_q.start()
-            swap_do.start()
-
-    def ship(z1, d_key, d_value):
-        for r in range(np):
+            for copy in swap_qd:
+                copy.start()
+
+    def ship(z1, d_key, d_value, pieces):
+        for r in pieces:
             fsend[z1, r, 0] = d_key[r * half:(r + 1) * half].astype(BF16)
             fsend[z1, r, 1] = d_value[r * half:(r + 1) * half].astype(BF16)
 
     def later(r):
         def step(z1, _):
-            @pl.when(z1 < z)
+            sent = ((z1 == 0) & (early | (z > 1))) if r == 1 else z1 < 0
+
+            @pl.when((z1 < z) & jnp.logical_not(sent))
             def _():
                 fin_copy(r, z1).start()
             return 0
         lax.fori_loop(0, zs, step, 0)
 
+    def last_pieces():
+        for r in range(2, np):
+            later(r)
+
     def swapped():
         dqt[1] = jnp.zeros_like(dqt[1])
         with jax.named_scope("wait_swap"):
-            swap_q.wait_recv()
-            swap_do.wait_recv()
             swap_stats.wait_recv()
-        stack(1, pair_qd)
+            for copy in swap_qd:
+                copy.wait_recv()
+
+    def leave(z1, d_key, d_value):
+        ship(z1, d_key, d_value, range(1))
+        fin_copy(0, z1).start()
+        ship(z1, d_key, d_value, range(1, np))
 
     def pair_tile(z1):
         with jax.named_scope("pair_tile"):
             d_key, d_value = tile(1, kv[z1, 0], kv[z1, 1], 2 * z1 + y, False)
-            ship(z1, part[z1, 0] + d_key, part[z1, 1] + d_value)
-        fin_copy(0, z1).start()
-
-    pl.when(early)(swapped)
+            leave(z1, part[z1, 0] + d_key, part[z1, 1] + d_value)
+
+        @pl.when(((z1 == 0) & early) | ((z1 == 1) & late))
+        def _():
+            fin_copy(1, 0).start()
 
     def own_step(z1, _):
         @pl.when((z1 < z) | ((z1 == zs) & (z == 0) & (y == 1)))
@@ -288,6 +304,8 @@
                 part[z1, 0] = d_key
                 part[z1, 1] = d_value
 
+        pl.when((z1 == 0) & early)(swapped)
+
         @pl.when((z1 < z) & early)
         def _():
             pair_tile(z1)
@@ -297,12 +315,12 @@
 
     @pl.when(early)
     def _():
-        for r in range(1, np):
-            later(r)
+        later(1)
+        pl.when(z == zs - 1)(last_pieces)
 
     @pl.when((z == 0) & (y == 1))
     def _():
-        ship(zs, part[zs, 0], part[zs, 1])
+        ship(zs, part[zs, 0], part[zs, 1], range(np))
         for r in range(np):
             pair_fin(r).start()
 
@@ -323,18 +341,18 @@
             return 0
 
         lax.fori_loop(0, zs, pair_step, 0)
-        for r in range(1, np):
-            later(r)
+        later(1)
+        pl.when(z == zs - 1)(last_pieces)
+
+    @pl.when(swapping & (y == 0))
+    def _():
+        with jax.named_scope("pair_own"):
+            d_key, d_value = tile(1, own[0], own[1], me, False)
+            acc[0] += d_key
+            acc[1] += d_value
 
     @pl.when(swapping)
     def _():
-        @pl.when(y == 0)
-        def _():
-            with jax.named_scope("pair_own"):
-                d_key, d_value = tile(1, own[0], own[1], me, False)
-                acc[0] += d_key
-                acc[1] += d_value
-
         pair_dq = jnp.transpose(dqt[1]).astype(BF16)
         for r in range(np):
             for g in range(group):
@@ -348,9 +366,12 @@
     def g_copy(r):
         return remote(gs.at[0, r], gs.at[1, r], g_send.at[0], g_recv.at[r], heads=other)
 
+    def side(c, dx, s, n, r):
+        cols = slice(dx * mine + s * width, dx * mine + (s + n) * width)
+        return dot(gs[c, r], w[c, cols, :], NT)
+
     def whole(dx, s, n, r):
-        cols = slice(dx * mine + s * width, dx * mine + (s + n) * width)
-        return dot(gs[0, r], w[0, cols, :], NT) + dot(gs[1, r], w[1, cols, :], NT)
+        return side(0, dx, s, n, r) + side(1, dx, s, n, r)
 
     def cross_copy(dx, r, i):
         at = (dx - 1, r, pl.ds(*plan[r][i]))
@@ -362,7 +383,7 @@
         rows = slice(r * half, (r + 1) * half)
 
         def collect(i, _):
-            z2 = zs - i
+            z2 = lax.rem(i + zs, zs + 1)
 
             @pl.when(((z2 > z) & (z2 < zs)) | ((z2 == zs) & (z == 0) & (y == 0)))
             def _():
@@ -374,6 +395,8 @@
             @pl.when(swapping)
             def _():
                 swap_dq(r).wait_recv()
+        if r == 0:
+            pl.when(z < zs - 1)(last_pieces)
         for g in range(group):
             total = dq_own[g * cap + r * half:g * cap + (r + 1) * half, :] + dq_recv[r, g].astype(F32)
             gs[0, r, :, g * dim:(g + 1) * dim] = (total * scale).astype(BF16)
@@ -381,20 +404,48 @@
             lax.fori_loop(0, zs + 1, collect, 0)
         key_total = acc[0, rows, :] * scale
         value_total = acc[1, rows, :]
-        dk_ref[rows, :] = key_total
-        dv_ref[rows, :] = value_total
         gs[0, r, :, wide:wide + dim] = key_total.astype(BF16)
         gs[0, r, :, wide + dim:wide + 2 * dim] = value_total.astype(BF16)
         g_copy(r).start()
-        with jax.named_scope("wait_g"):
-            g_copy(r).wait_recv()
-        with jax.named_scope("project"):
-            for dx in range(1, nx):
-                for i, (s, n) in enumerate(plan[r]):
-                    terms = whole(dx, s, n, r).astype(BF16)
-                    for j in range(n):
-                        xsend[dx - 1, r, s + j] = terms[:, j * width:(j + 1) * width]
-                    cross_copy(dx, r, i).start()
+        dk_ref[rows, :] = key_total
+        dv_ref[rows, :] = value_total
+        blocks = [(dx, i) for dx in range(1, nx) for i in range(len(plan[r]))]
+
+        def half_sum(dx, i):
+            s, n = plan[r][i]
+            keep[dx - 1, :, s * width:(s + n) * width] = side(0, dx, s, n, r)
+
+        def finish(dx, i):
+            s, n = plan[r][i]
+            terms = keep[dx - 1, :, s * width:(s + n) * width] + side(1, dx, s, n, r)
+            terms = terms.astype(BF16)
+            for j in range(n):
+                xsend[dx - 1, r, s + j] = terms[:, j * width:(j + 1) * width]
+            cross_copy(dx, r, i).start()
+
+        def waiting():
+            with jax.named_scope("half"):
+                for dx, i in blocks:
+                    half_sum(dx, i)
+            with jax.named_scope("wait_g"):
+                g_copy(r).wait_recv()
+            with jax.named_scope("project"):
+                for dx, i in blocks:
+                    finish(dx, i)
+
+        def ready():
+            with jax.named_scope("wait_g"):
+                g_copy(r).wait_recv()
+            with jax.named_scope("project"):
+                for dx, i in blocks:
+                    half_sum(dx, i)
+                    finish(dx, i)
+
+        if r == 0:
+            pl.when(core == 0)(waiting)
+            pl.when(core == 1)(ready)
+        else:
+            waiting()
     with jax.named_scope("own_proj"):
         for r in range(np):
             for s in range(0, ns, 2):
@@ -413,13 +464,17 @@
                 out_ref[rows, cols] = total.astype(BF16)
 
     with jax.named_scope("drain"):
-        pl.when(late)(swap_q.wait_send)
+        @pl.when(late)
+        def _():
+            for copy in swap_qd[:group // 2]:
+                copy.wait_send()
 
         @pl.when(swapping)
         def _():
-            swap_do.wait_send()
+            for copy in swap_qd[group // 2:]:
+                copy.wait_send()
             swap_stats.wait_send()
-            remote(dq_send, dq_recv, swap_send.at[2], swap_recv.at[2], ctx=pair).wait_send()
+            remote(dq_send, dq_recv, swap_send.at[group + 1], swap_recv.at[group + 1], ctx=pair).wait_send()
 
         def fins_sent(z1):
             remote(fsend.at[z1], frcv.at[z1], f_send.at[z1], f_recv.at[z1, 0], ctx=pair).wait_send()
@@ -452,11 +507,14 @@
             ).wait_send()
 
 
-def emit(a, b, c, a_hbm, b_hbm, c_hbm, sem):
-    copies = [
-        pltpu.make_async_copy(src, dst, sem.at[i])
-        for i, (src, dst) in enumerate(((a, a_hbm), (b, b_hbm), (c, c_hbm)))
-    ]
+def emit(parts, *refs):
+    sem = refs[-1]
+    copies = []
+    for src, dst, n in zip(refs, refs[len(parts):], parts):
+        step = src.shape[0] // n
+        for i in range(n):
+            at = pl.ds(i * step, step)
+            copies.append(pltpu.make_async_copy(src.at[at], dst.at[at], sem.at[len(copies)]))
     for copy in copies:
         copy.start()
     for copy in copies:
@@ -492,13 +550,10 @@
         scratch_shapes=[
             pltpu.SMEM(block_counts.shape, jnp.int32),
             pltpu.VMEM((2, cap, dim), BF16),
-            pltpu.VMEM((2, cap, width), BF16),
-            pltpu.VMEM((cap, width), BF16),
+            pltpu.VMEM((2, width // dim, 2, cap, dim), BF16),
+            pltpu.VMEM((width // dim, cap, dim), BF16),
             pltpu.VMEM(log_sum_exp.shape, F32),
-            pltpu.VMEM((2, cap, width), BF16),
             pltpu.VMEM((2, nx * mine, width + 2 * dim), BF16),
-            pltpu.VMEM((2, rows, dim), BF16),
-            pltpu.VMEM((2, rows, dim), BF16),
             pltpu.VMEM((2, 2, rows), F32),
             pltpu.VMEM((2, dim, rows), F32),
             pltpu.VMEM((rows, dim), F32),
@@ -510,6 +565,7 @@
             pltpu.VMEM((zs + 1, 2, cap, dim), F32),
             pltpu.VMEM((zs + 1, np, 2, half, dim), BF16),
             pltpu.VMEM((zs + 1, np, 2, half, dim), BF16),
+            pltpu.VMEM((nx - 1, half, mine), F32),
             pltpu.VMEM((cap, mine), F32),
             pltpu.VMEM((nx - 1, np, ns, half, chunk), BF16),
             pltpu.VMEM((nx - 1, np, ns, half, chunk), BF16),
@@ -519,8 +575,8 @@
             dma((1,)),
             dma((zs + 1,)),
             dma((zs + 1,)),
-            dma((4,)),
-            dma((3 + np,)),
+            dma((width // dim + 2,)),
+            dma((width // dim + 1 + np,)),
             dma((zs + 1,)),
             dma((zs + 1, np)),
             dma((1,)),
@@ -542,11 +598,11 @@
         )
     )
     return pl.pallas_call(
-        emit,
+        functools.partial(emit, (EMIT, 1, 1)),
         out_shape=tuple(jax.ShapeDtypeStruct(a.shape, a.dtype) for a in results),
         in_specs=[vmem] * 3,
         out_specs=(hbm,) * 3,
-        scratch_shapes=[dma((3,))],
+        scratch_shapes=[dma((EMIT + 2,))],
     )(*(pltpu.with_memory_space_constraint(a, pltpu.VMEM) for a in results))
 
 

time: 34.6 us -> 34 us (0.983)
  Pallas kernels: 33.8 us -> 33.2 us
    pallas_call x1, Pallas kernels: 33 us -> 32.3 us  [on_device(): pl.pallas_call(functools.partial(kernel, zs, nx, ns), out_shape=(jax.Shap...]
where the time goes in v3:
time: 34 us; the launch traced here: 33.8 us
  Pallas kernels  33.2 us (98%)
  between operations  0.64 us (2%)
    pallas_call x1, Pallas kernels, on_device(): pl.pallas_call(functools.partial(kernel, zs, nx, ns), out_shape=(jax.Shap...  32.3 us
    pallas_call x1, Pallas kernels, on_device(): pl.pallas_call(functools.partial(emit, (EMIT, 1, 1)), out_shape=tuple((ja...  0.86 us

profile of v3, /device:TPU:0, one launch (start us, length us, event | category | flops | bytes accessed | tf_op | source)
XLA Modules:
  0.0 33.8 jit_solution(15882940040757583797)
XLA Ops:
  0.6 32.3 %shard_map.121 = (bf16[192,1024]{1,0:T(8,128)(2,1)S(1)}, f32[192,128]{1,0:T(8,128)S(1)}, f32[192,128]{1,0:T(8,128)S(1)}) custom-call(bf16[192,512]{1,0:T(8,128)(2,1)} %q_hbm.1, bf16[192,128]{1,0:T(8,128)(2,1)} %k_hbm.1, bf16[192,128]{1,0:T(8,128)(2,1)} %v_hbm.1, bf16[192,512]{1,0:T(8,128)(2,1)} %o_hbm.1, bf16[192,512]{1,0:T(8,128)(2,1)} %do_hbm.1, ...), custom_call_target="tpu_custom_call" | custom-call | tf_op jit(solution)/shard_map/pallas_call | solution.py:541
  33.0 0.9 %shard_map.122 = (bf16[192,1024]{1,0:T(8,128)(2,1)}, f32[192,128]{1,0:T(8,128)}, f32[192,128]{1,0:T(8,128)}) custom-call(bf16[192,1024]{1,0:T(8,128)(2,1)S(1)} %get-tuple-element.6.refs_0_, f32[192,128]{1,0:T(8,128)S(1)} %get-tuple-element.7.refs_1_, f32[192,128]{1,0:T(8,128)S(1)} %get-tuple-element.8.refs_2_), custom_call_target="tpu_custom_call" | custom-call | tf_op jit(solution)/shard_map/pallas_call | solution.py:600

commit v4 on v3

--- a/solution.py
+++ b/solution.py
@@ -9,7 +9,7 @@
 from jax.sharding import PartitionSpec as P
 
 BLOCK = 64
-EMIT = 4
+EMIT = 2
 LOG2E = math.log2(math.e)
 F32 = jnp.float32
 BF16 = jnp.bfloat16
@@ -33,14 +33,14 @@
     return plan
 
 
-def kernel(
+def body(
     zs, nx, ns,
     q_hbm, k_hbm, v_hbm, o_hbm, do_hbm, lse_hbm, cnt_hbm, wq_hbm, wk_hbm, wv_hbm,
     out_ref, dk_ref, dv_ref,
     cnt_ref, own, qd, o_ref, lse_ref, w, stats, dqt,
     dq_own, dq_send, dq_recv, gs, acc, kv, part, fsend, frcv, keep, hold, xsend, xrcv,
-    in_sem, w_sem, w_send, w_recv, own_send, kv_recv, swap_send, swap_recv, f_send, f_recv,
-    g_send, g_recv, x_send, x_recv, turn,
+    w_recv, kv_recv, swap_recv, f_recv, g_recv, x_recv, turn,
+    in_sem, w_sem, w_send, own_send, swap_send, f_send, g_send, x_send,
 ):
     cap, dim = own.shape[1:]
     group = qd.shape[1]
@@ -57,7 +57,8 @@
     core = lax.rem(h, 2)
     x = lax.div(h, 2)
     other = h + 1 - 2 * core
-    across = [2 * lax.rem(x + dx, nx) + core for dx in range(nx)]
+    across = [h] + [2 * lax.rem(x + dx, nx) + 1 - core for dx in range(1, nx)]
+    theirs = [other] + [2 * lax.rem(x + dx, nx) + core for dx in range(1, nx)]
 
     def remote(src, dst, send, recv, **device):
         return pltpu.make_async_remote_copy(
@@ -81,7 +82,7 @@
     ]
     w_shares = [
         remote(
-            w_rows(across[dx] + 1 - 2 * core, src), w.at[1, pl.ds(dx * mine, mine), pl.ds(at, size)],
+            w_rows(theirs[dx], src), w.at[1, pl.ds(dx * mine, mine), pl.ds(at, size)],
             w_send.at[0], w_recv.at[0], heads=other,
         )
         for dx in range(nx)
@@ -132,7 +133,7 @@
     def own_copy(z2):
         return remote(own, kv.at[z], own_send.at[z2], kv_recv.at[z], ctx=2 * z2 + y)
 
-    pair_own_copy = remote(own, kv.at[zs], own_send.at[zs], kv_recv.at[zs], ctx=pair)
+    pair_own_copy = remote(own, kv.at[zs - 1], own_send.at[0], kv_recv.at[zs - 1], ctx=pair)
 
     def arrived(z1):
         remote(kv.at[z1], kv.at[z1], own_send.at[z1], kv_recv.at[z1], ctx=pair).wait_recv()
@@ -157,7 +158,7 @@
 
     def pair_fin(r):
         return remote(
-            fsend.at[zs, r], frcv.at[zs, r], f_send.at[zs], f_recv.at[zs, r], ctx=pair
+            fsend.at[zs - 1, r], frcv.at[0, r], f_send.at[zs - 1], f_recv.at[0, r], ctx=pair
         )
 
     def fin_wait(r, z2):
@@ -294,12 +295,12 @@
             fin_copy(1, 0).start()
 
     def own_step(z1, _):
-        @pl.when((z1 < z) | ((z1 == zs) & (z == 0) & (y == 1)))
+        @pl.when((z1 < z) | ((z1 == zs - 1) & (z == 0) & (y == 1)))
         def _():
             with jax.named_scope("wait_kv"):
                 arrived(z1)
             with jax.named_scope("own_tile"):
-                b = jnp.where(z1 == zs, pair, 2 * z1 + y)
+                b = jnp.where(z == 0, pair, 2 * z1 + y)
                 d_key, d_value = tile(0, kv[z1, 0], kv[z1, 1], b, False)
                 part[z1, 0] = d_key
                 part[z1, 1] = d_value
@@ -311,7 +312,7 @@
             pair_tile(z1)
         return 0
 
-    lax.fori_loop(0, zs + 1, own_step, 0)
+    lax.fori_loop(0, zs, own_step, 0)
 
     @pl.when(early)
     def _():
@@ -320,7 +321,7 @@
 
     @pl.when((z == 0) & (y == 1))
     def _():
-        ship(zs, part[zs, 0], part[zs, 1], range(np))
+        ship(zs - 1, part[zs - 1, 0], part[zs - 1, 1], range(np))
         for r in range(np):
             pair_fin(r).start()
 
@@ -363,8 +364,11 @@
     remote(w.at[1], w.at[1], w_send.at[0], w_recv.at[0], heads=other).wait_recv()
     width = mine // ns
 
-    def g_copy(r):
-        return remote(gs.at[0, r], gs.at[1, r], g_send.at[0], g_recv.at[r], heads=other)
+    def g_copy(r, at=0, size=None):
+        columns = pl.ds(at, wide + 2 * dim if size is None else size)
+        return remote(
+            gs.at[0, r, :, columns], gs.at[1, r, :, columns], g_send.at[0], g_recv.at[r], heads=other
+        )
 
     def side(c, dx, s, n, r):
         cols = slice(dx * mine + s * width, dx * mine + (s + n) * width)
@@ -382,10 +386,8 @@
     for r in range(np):
         rows = slice(r * half, (r + 1) * half)
 
-        def collect(i, _):
-            z2 = lax.rem(i + zs, zs + 1)
-
-            @pl.when(((z2 > z) & (z2 < zs)) | ((z2 == zs) & (z == 0) & (y == 0)))
+        def collect(z2, _):
+            @pl.when((z2 > z) | ((z2 == 0) & (z == 0) & (y == 0)))
             def _():
                 fin_wait(r, z2)
                 acc[:, rows, :] += frcv[z2, r].astype(F32)
@@ -400,13 +402,14 @@
         for g in range(group):
             total = dq_own[g * cap + r * half:g * cap + (r + 1) * half, :] + dq_recv[r, g].astype(F32)
             gs[0, r, :, g * dim:(g + 1) * dim] = (total * scale).astype(BF16)
+        g_copy(r, 0, wide).start()
         with jax.named_scope("collect"):
-            lax.fori_loop(0, zs + 1, collect, 0)
+            lax.fori_loop(0, zs, collect, 0)
         key_total = acc[0, rows, :] * scale
         value_total = acc[1, rows, :]
         gs[0, r, :, wide:wide + dim] = key_total.astype(BF16)
         gs[0, r, :, wide + dim:wide + 2 * dim] = value_total.astype(BF16)
-        g_copy(r).start()
+        g_copy(r, wide, 2 * dim).start()
         dk_ref[rows, :] = key_total
         dv_ref[rows, :] = value_total
         blocks = [(dx, i) for dx in range(1, nx) for i in range(len(plan[r]))]
@@ -497,7 +500,7 @@
 
         @pl.when((z == 0) & (y == 1))
         def _():
-            fins_sent(zs)
+            fins_sent(zs - 1)
 
         remote(w.at[1], w.at[1], w_send.at[0], w_recv.at[0], heads=other).wait_send()
         remote(gs.at[0], gs.at[1], g_send.at[0], g_recv.at[0], heads=other).wait_send()
@@ -505,6 +508,15 @@
             remote(
                 xsend.at[dx - 1], xrcv.at[dx - 1], x_send.at[0], x_recv.at[dx - 1, 0], heads=across[dx]
             ).wait_send()
+
+
+def kernel(zs, nx, ns, group, *refs):
+    dma = pltpu.SemaphoreType.DMA
+    pl.run_scoped(
+        functools.partial(body, zs, nx, ns, *refs),
+        in_sem=dma((5,)), w_sem=dma((1,)), w_send=dma((1,)), own_send=dma((zs,)),
+        swap_send=dma((group + 2,)), f_send=dma((zs,)), g_send=dma((1,)), x_send=dma((1,)),
+    )
 
 
 def emit(parts, *refs):
@@ -539,7 +551,7 @@
     hbm = pl.BlockSpec(memory_space=pltpu.HBM)
     dma = pltpu.SemaphoreType.DMA
     results = pl.pallas_call(
-        functools.partial(kernel, zs, nx, ns),
+        functools.partial(kernel, zs, nx, ns, width // dim),
         out_shape=(
             jax.ShapeDtypeStruct((cap, mine), BF16),
             jax.ShapeDtypeStruct((cap, dim), F32),
@@ -561,27 +573,19 @@
             pltpu.VMEM((np, width // dim, half, dim), BF16),
             pltpu.VMEM((2, np, half, width + 2 * dim), BF16),
             pltpu.VMEM((2, cap, dim), F32),
-            pltpu.VMEM((zs + 1, 2, cap, dim), BF16),
-            pltpu.VMEM((zs + 1, 2, cap, dim), F32),
-            pltpu.VMEM((zs + 1, np, 2, half, dim), BF16),
-            pltpu.VMEM((zs + 1, np, 2, half, dim), BF16),
+            pltpu.VMEM((zs, 2, cap, dim), BF16),
+            pltpu.VMEM((zs, 2, cap, dim), F32),
+            pltpu.VMEM((zs, np, 2, half, dim), BF16),
+            pltpu.VMEM((zs, np, 2, half, dim), BF16),
             pltpu.VMEM((nx - 1, half, mine), F32),
             pltpu.VMEM((cap, mine), F32),
             pltpu.VMEM((nx - 1, np, ns, half, chunk), BF16),
             pltpu.VMEM((nx - 1, np, ns, half, chunk), BF16),
-            dma((5,)),
             dma((1,)),
-            dma((1,)),
-            dma((1,)),
-            dma((zs + 1,)),
-            dma((zs + 1,)),
-            dma((width // dim + 2,)),
+            dma((zs,)),
             dma((width // dim + 1 + np,)),
-            dma((zs + 1,)),
-            dma((zs + 1, np)),
-            dma((1,)),
+            dma((zs, np)),
             dma((np,)),
-            dma((1,)),
             dma((nx - 1, blocks)),
             pltpu.SemaphoreType.REGULAR,
         ],

time: 34 us -> 33.4 us (0.982)
  Pallas kernels: 33.2 us -> 32.6 us
    pallas_call x1, Pallas kernels: 32.3 us -> 31.7 us  [on_device(): pl.pallas_call(functools.partial(kernel, zs, nx, ns, width // dim), out_s...]
where the time goes in v4:
time: 33.4 us; the launch traced here: 33.2 us
  Pallas kernels  32.6 us (98%)
  between operations  0.64 us (2%)
    pallas_call x1, Pallas kernels, on_device(): pl.pallas_call(functools.partial(kernel, zs, nx, ns, width // dim), out_s...  31.7 us
    pallas_call x1, Pallas kernels, on_device(): pl.pallas_call(functools.partial(emit, (EMIT, 1, 1)), out_shape=tuple((ja...  0.84 us

profile of v4, /device:TPU:0, one launch (start us, length us, event | category | flops | bytes accessed | tf_op | source)
XLA Modules:
  0.0 33.2 jit_solution(16466811648669744447)
XLA Ops:
  0.6 31.7 %shard_map.121 = (bf16[192,1024]{1,0:T(8,128)(2,1)S(1)}, f32[192,128]{1,0:T(8,128)S(1)}, f32[192,128]{1,0:T(8,128)S(1)}) custom-call(bf16[192,512]{1,0:T(8,128)(2,1)} %refs_0_.1, bf16[192,128]{1,0:T(8,128)(2,1)} %refs_1_.1, bf16[192,128]{1,0:T(8,128)(2,1)} %refs_2_.1, bf16[192,512]{1,0:T(8,128)(2,1)} %refs_3_.1, bf16[192,512]{1,0:T(8,128)(2,1)} %refs_4_.1, ...), custom_call_target="tpu_custom_call" | custom-call | tf_op jit(solution)/shard_map/pallas_call | solution.py:553
  32.4 0.8 %shard_map.122 = (bf16[192,1024]{1,0:T(8,128)(2,1)}, f32[192,128]{1,0:T(8,128)}, f32[192,128]{1,0:T(8,128)}) custom-call(bf16[192,1024]{1,0:T(8,128)(2,1)S(1)} %get-tuple-element.6.refs_0_, f32[192,128]{1,0:T(8,128)S(1)} %get-tuple-element.7.refs_1_, f32[192,128]{1,0:T(8,128)S(1)} %get-tuple-element.8.refs_2_), custom_call_target="tpu_custom_call" | custom-call | tf_op jit(solution)/shard_map/pallas_call | solution.py:604

commit v5 on v4

--- a/solution.py
+++ b/solution.py
@@ -37,7 +37,7 @@
     zs, nx, ns,
     q_hbm, k_hbm, v_hbm, o_hbm, do_hbm, lse_hbm, cnt_hbm, wq_hbm, wk_hbm, wv_hbm,
     out_ref, dk_ref, dv_ref,
-    cnt_ref, own, qd, o_ref, lse_ref, w, stats, dqt,
+    cnt_ref, own, qd, o_ref, lse_ref, w, wt, stats, dqt,
     dq_own, dq_send, dq_recv, gs, acc, kv, part, fsend, frcv, keep, hold, xsend, xrcv,
     w_recv, kv_recv, swap_recv, f_recv, g_recv, x_recv, turn,
     in_sem, w_sem, w_send, own_send, swap_send, f_send, g_send, x_send,
@@ -254,24 +254,35 @@
             for copy in swap_qd:
                 copy.start()
 
+    def turn_w(c):
+        def step(i, _):
+            at = pl.ds(pl.multiple_of(i * 256, 256), 256)
+            wt[c, :, at] = jnp.transpose(w[c, at, :])
+            return 0
+        with jax.named_scope("turn_w"):
+            lax.fori_loop(0, w.shape[1] // 256, step, 0)
+
+    pltpu.make_async_copy(w.at[0], w.at[0], w_sem.at[0]).wait()
+    turn_w(0)
+
     def ship(z1, d_key, d_value, pieces):
         for r in pieces:
             fsend[z1, r, 0] = d_key[r * half:(r + 1) * half].astype(BF16)
             fsend[z1, r, 1] = d_value[r * half:(r + 1) * half].astype(BF16)
 
-    def later(r):
+    def later(pieces):
         def step(z1, _):
-            sent = ((z1 == 0) & (early | (z > 1))) if r == 1 else z1 < 0
-
-            @pl.when((z1 < z) & jnp.logical_not(sent))
-            def _():
-                fin_copy(r, z1).start()
+            for r in pieces:
+                sent = ((z1 == 0) & (early | (z > 1))) if r < np - 1 else z1 < 0
+
+                @pl.when((z1 < z) & jnp.logical_not(sent))
+                def _():
+                    fin_copy(r, z1).start()
             return 0
         lax.fori_loop(0, zs, step, 0)
 
     def last_pieces():
-        for r in range(2, np):
-            later(r)
+        later([np - 1])
 
     def swapped():
         dqt[1] = jnp.zeros_like(dqt[1])
@@ -292,7 +303,8 @@
 
         @pl.when(((z1 == 0) & early) | ((z1 == 1) & late))
         def _():
-            fin_copy(1, 0).start()
+            for r in range(1, np - 1):
+                fin_copy(r, 0).start()
 
     def own_step(z1, _):
         @pl.when((z1 < z) | ((z1 == zs - 1) & (z == 0) & (y == 1)))
@@ -316,7 +328,7 @@
 
     @pl.when(early)
     def _():
-        later(1)
+        later(range(1, np - 1))
         pl.when(z == zs - 1)(last_pieces)
 
     @pl.when((z == 0) & (y == 1))
@@ -342,7 +354,7 @@
             return 0
 
         lax.fori_loop(0, zs, pair_step, 0)
-        later(1)
+        later(range(1, np - 1))
         pl.when(z == zs - 1)(last_pieces)
 
     @pl.when(swapping & (y == 0))
@@ -360,8 +372,6 @@
                 dq_send[r, g] = pair_dq[g * cap + r * half:g * cap + (r + 1) * half]
             swap_dq(r).start()
 
-    pltpu.make_async_copy(w.at[0], w.at[0], w_sem.at[0]).wait()
-    remote(w.at[1], w.at[1], w_send.at[0], w_recv.at[0], heads=other).wait_recv()
     width = mine // ns
 
     def g_copy(r, at=0, size=None):
@@ -372,7 +382,7 @@
 
     def side(c, dx, s, n, r):
         cols = slice(dx * mine + s * width, dx * mine + (s + n) * width)
-        return dot(gs[c, r], w[c, cols, :], NT)
+        return dot(gs[c, r], wt[c, :, cols])
 
     def whole(dx, s, n, r):
         return side(0, dx, s, n, r) + side(1, dx, s, n, r)
@@ -382,6 +392,9 @@
         return remote(
             xsend.at[at], xrcv.at[at], x_send.at[0], x_recv.at[dx - 1, first[r] + i], heads=across[dx]
         )
+
+    remote(w.at[1], w.at[1], w_send.at[0], w_recv.at[0], heads=other).wait_recv()
+    turn_w(1)
 
     for r in range(np):
         rows = slice(r * half, (r + 1) * half)
@@ -545,7 +558,7 @@
     mine = model // nh
     chunk = mine // ns
     vmem = pl.BlockSpec(memory_space=pltpu.VMEM)
-    half = BLOCK
+    half = cap // 4
     np = cap // half
     blocks = sum(len(p) for p in row_blocks(np, ns))
     hbm = pl.BlockSpec(memory_space=pltpu.HBM)
@@ -566,6 +579,7 @@
             pltpu.VMEM((width // dim, cap, dim), BF16),
             pltpu.VMEM(log_sum_exp.shape, F32),
             pltpu.VMEM((2, nx * mine, width + 2 * dim), BF16),
+            pltpu.VMEM((2, width + 2 * dim, nx * mine), BF16),
             pltpu.VMEM((2, 2, rows), F32),
             pltpu.VMEM((2, dim, rows), F32),
             pltpu.VMEM((rows, dim), F32),

time: 33.4 us -> 33.1 us (level)
  Pallas kernels: 32.6 us -> 32.2 us
where the time goes in v5:
time: 33.1 us; the launch traced here: 32.9 us
  Pallas kernels  32.2 us (97%)
  between operations  0.64 us (2%)
    pallas_call x1, Pallas kernels, on_device(): pl.pallas_call(functools.partial(kernel, zs, nx, ns, width // dim), out_s...  31.4 us
    pallas_call x1, Pallas kernels, on_device(): pl.pallas_call(functools.partial(emit, (EMIT, 1, 1)), out_shape=tuple((ja...  0.84 us

profile of v5, /device:TPU:0, one launch (start us, length us, event | category | flops | bytes accessed | tf_op | source)
XLA Modules:
  0.0 32.9 jit_solution(12248226220078430360)
XLA Ops:
  0.6 31.4 %shard_map.121 = (bf16[192,1024]{1,0:T(8,128)(2,1)S(1)}, f32[192,128]{1,0:T(8,128)S(1)}, f32[192,128]{1,0:T(8,128)S(1)}) custom-call(bf16[192,512]{1,0:T(8,128)(2,1)} %refs_0_.1, bf16[192,128]{1,0:T(8,128)(2,1)} %refs_1_.1, bf16[192,128]{1,0:T(8,128)(2,1)} %refs_2_.1, bf16[192,512]{1,0:T(8,128)(2,1)} %refs_3_.1, bf16[192,512]{1,0:T(8,128)(2,1)} %refs_4_.1, ...), custom_call_target="tpu_custom_call" | custom-call | tf_op jit(solution)/shard_map/pallas_call | solution.py:566
  32.0 0.8 %shard_map.122 = (bf16[192,1024]{1,0:T(8,128)(2,1)}, f32[192,128]{1,0:T(8,128)}, f32[192,128]{1,0:T(8,128)}) custom-call(bf16[192,1024]{1,0:T(8,128)(2,1)S(1)} %get-tuple-element.6.refs_0_, f32[192,128]{1,0:T(8,128)S(1)} %get-tuple-element.7.refs_1_, f32[192,128]{1,0:T(8,128)S(1)} %get-tuple-element.8.refs_2_), custom_call_target="tpu_custom_call" | custom-call | tf_op jit(solution)/shard_map/pallas_call | solution.py:618

commit v6 on v5

--- a/solution.py
+++ b/solution.py
@@ -241,7 +241,7 @@
     @pl.when(early)
     def _():
         with jax.named_scope("hand_over"):
-            for copy in swap_qd[:group // 2]:
+            for copy in swap_qd[:3]:
                 copy.wait_send()
             pl.semaphore_signal(
                 turn, inc=1, device_id={"heads": other}, device_id_type=pl.DeviceIdType.MESH
@@ -273,7 +273,7 @@
     def later(pieces):
         def step(z1, _):
             for r in pieces:
-                sent = ((z1 == 0) & (early | (z > 1))) if r < np - 1 else z1 < 0
+                sent = ((z1 == 0) & (early | ((z > 1) if r == 1 else False))) if r < np - 1 else z1 < 0
 
                 @pl.when((z1 < z) & jnp.logical_not(sent))
                 def _():
@@ -303,7 +303,11 @@
 
         @pl.when(((z1 == 0) & early) | ((z1 == 1) & late))
         def _():
-            for r in range(1, np - 1):
+            fin_copy(1, 0).start()
+
+        @pl.when((z1 == 0) & early)
+        def _():
+            for r in range(2, np - 1):
                 fin_copy(r, 0).start()
 
     def own_step(z1, _):
@@ -482,12 +486,12 @@
     with jax.named_scope("drain"):
         @pl.when(late)
         def _():
-            for copy in swap_qd[:group // 2]:
+            for copy in swap_qd[:3]:
                 copy.wait_send()
 
         @pl.when(swapping)
         def _():
-            for copy in swap_qd[group // 2:]:
+            for copy in swap_qd[3:]:
                 copy.wait_send()
             swap_stats.wait_send()
             remote(dq_send, dq_recv, swap_send.at[group + 1], swap_recv.at[group + 1], ctx=pair).wait_send()

time: 33.1 us -> 32.9 us (level)
    pallas_call x1, Pallas kernels: 31.4 us -> 31 us  [on_device(): pl.pallas_call(functools.partial(kernel, zs, nx, ns, width // dim), out_s...]
where the time goes in v6:
time: 32.9 us; the launch traced here: 32.5 us
  Pallas kernels  31.9 us (97%)
  between operations  0.64 us (2%)
    pallas_call x1, Pallas kernels, on_device(): pl.pallas_call(functools.partial(kernel, zs, nx, ns, width // dim), out_s...  31 us
    pallas_call x1, Pallas kernels, on_device(): pl.pallas_call(functools.partial(emit, (EMIT, 1, 1)), out_shape=tuple((ja...  0.84 us

profile of v6, /device:TPU:0, one launch (start us, length us, event | category | flops | bytes accessed | tf_op | source)
XLA Modules:
  0.0 32.5 jit_solution(16234811945360414795)
XLA Ops:
  0.6 31.0 %shard_map.121 = (bf16[192,1024]{1,0:T(8,128)(2,1)S(1)}, f32[192,128]{1,0:T(8,128)S(1)}, f32[192,128]{1,0:T(8,128)S(1)}) custom-call(bf16[192,512]{1,0:T(8,128)(2,1)} %refs_0_.1, bf16[192,128]{1,0:T(8,128)(2,1)} %refs_1_.1, bf16[192,128]{1,0:T(8,128)(2,1)} %refs_2_.1, bf16[192,512]{1,0:T(8,128)(2,1)} %refs_3_.1, bf16[192,512]{1,0:T(8,128)(2,1)} %refs_4_.1, ...), custom_call_target="tpu_custom_call" | custom-call | tf_op jit(solution)/shard_map/pallas_call | solution.py:570
  31.7 0.8 %shard_map.122 = (bf16[192,1024]{1,0:T(8,128)(2,1)}, f32[192,128]{1,0:T(8,128)}, f32[192,128]{1,0:T(8,128)}) custom-call(bf16[192,1024]{1,0:T(8,128)(2,1)S(1)} %get-tuple-element.6.refs_0_, f32[192,128]{1,0:T(8,128)S(1)} %get-tuple-element.7.refs_1_, f32[192,128]{1,0:T(8,128)S(1)} %get-tuple-element.8.refs_2_), custom_call_target="tpu_custom_call" | custom-call | tf_op jit(solution)/shard_map/pallas_call | solution.py:622

commit v7 on v6

--- a/solution.py
+++ b/solution.py
@@ -139,16 +139,16 @@
         remote(kv.at[z1], kv.at[z1], own_send.at[z1], kv_recv.at[z1], ctx=pair).wait_recv()
 
     swap_qd = [
-        remote(qd.at[0, g], qd.at[1, g], swap_send.at[g], swap_recv.at[g], ctx=pair)
+        remote(qd.at[0, g], qd.at[1, g], swap_send.at[g], swap_recv.at[0], ctx=pair)
         for g in range(group)
     ]
     swap_stats = remote(
-        stats.at[0], stats.at[1], swap_send.at[group], swap_recv.at[group], ctx=pair
+        stats.at[0], stats.at[1], swap_send.at[group], swap_recv.at[1], ctx=pair
     )
 
     def swap_dq(r):
         return remote(
-            dq_send.at[r], dq_recv.at[r], swap_send.at[group + 1], swap_recv.at[group + 1 + r], ctx=pair
+            dq_send.at[r], dq_recv.at[r], swap_send.at[group + 1], swap_recv.at[2 + r], ctx=pair
         )
 
     def fin_copy(r, z1):
@@ -288,8 +288,7 @@
         dqt[1] = jnp.zeros_like(dqt[1])
         with jax.named_scope("wait_swap"):
             swap_stats.wait_recv()
-            for copy in swap_qd:
-                copy.wait_recv()
+            remote(qd.at[0], qd.at[1], swap_send.at[0], swap_recv.at[0], ctx=pair).wait_recv()
 
     def leave(z1, d_key, d_value):
         ship(z1, d_key, d_value, range(1))
@@ -394,7 +393,7 @@
     def cross_copy(dx, r, i):
         at = (dx - 1, r, pl.ds(*plan[r][i]))
         return remote(
-            xsend.at[at], xrcv.at[at], x_send.at[0], x_recv.at[dx - 1, first[r] + i], heads=across[dx]
+            xsend.at[at], xrcv.at[at], x_send.at[0], x_recv.at[dx - 1, r + i * (r == np - 1)], heads=across[dx]
         )
 
     remote(w.at[1], w.at[1], w_send.at[0], w_recv.at[0], heads=other).wait_recv()
@@ -475,7 +474,13 @@
         for i, (s, n) in enumerate(plan[r]):
             for dx in range(1, nx):
                 with jax.named_scope("wait_cross"):
-                    cross_copy(dx, r, i).wait_recv()
+                    if r == np - 1:
+                        cross_copy(dx, r, i).wait_recv()
+                    elif i == 0:
+                        remote(
+                            xsend.at[dx - 1, r], xrcv.at[dx - 1, r], x_send.at[0], x_recv.at[dx - 1, r],
+                            heads=across[dx],
+                        ).wait_recv()
             for j in range(s, s + n):
                 cols = slice(j * width, (j + 1) * width)
                 total = hold[rows, cols]
@@ -494,7 +499,7 @@
             for copy in swap_qd[3:]:
                 copy.wait_send()
             swap_stats.wait_send()
-            remote(dq_send, dq_recv, swap_send.at[group + 1], swap_recv.at[group + 1], ctx=pair).wait_send()
+            remote(dq_send, dq_recv, swap_send.at[group + 1], swap_recv.at[2], ctx=pair).wait_send()
 
         def fins_sent(z1):
             remote(fsend.at[z1], frcv.at[z1], f_send.at[z1], f_recv.at[z1, 0], ctx=pair).wait_send()
@@ -564,7 +569,7 @@
     vmem = pl.BlockSpec(memory_space=pltpu.VMEM)
     half = cap // 4
     np = cap // half
-    blocks = sum(len(p) for p in row_blocks(np, ns))
+    blocks = np - 1 + len(row_blocks(np, ns)[-1])
     hbm = pl.BlockSpec(memory_space=pltpu.HBM)
     dma = pltpu.SemaphoreType.DMA
     results = pl.pallas_call(
@@ -601,7 +606,7 @@
             pltpu.VMEM((nx - 1, np, ns, half, chunk), BF16),
             dma((1,)),
             dma((zs,)),
-            dma((width // dim + 1 + np,)),
+            dma((2 + np,)),
             dma((zs, np)),
             dma((np,)),
             dma((nx - 1, blocks)),

time: 32.9 us -> 32.9 us (level)
  no operation moved by 1% of the time
where the time goes in v7:
time: 32.9 us; the launch traced here: 32.5 us
  Pallas kernels  31.8 us (97%)
  between operations  0.64 us (2%)
    pallas_call x1, Pallas kernels, on_device(): pl.pallas_call(functools.partial(kernel, zs, nx, ns, width // dim), out_s...  31 us
    pallas_call x1, Pallas kernels, on_device(): pl.pallas_call(functools.partial(emit, (EMIT, 1, 1)), out_shape=tuple((ja...  0.84 us

profile of v7, /device:TPU:0, one launch (start us, length us, event | category | flops | bytes accessed | tf_op | source)
XLA Modules:
  0.0 32.5 jit_solution(17613656924045530113)
XLA Ops:
  0.6 31.0 %shard_map.121 = (bf16[192,1024]{1,0:T(8,128)(2,1)S(1)}, f32[192,128]{1,0:T(8,128)S(1)}, f32[192,128]{1,0:T(8,128)S(1)}) custom-call(bf16[192,512]{1,0:T(8,128)(2,1)} %refs_0_.1, bf16[192,128]{1,0:T(8,128)(2,1)} %refs_1_.1, bf16[192,128]{1,0:T(8,128)(2,1)} %refs_2_.1, bf16[192,512]{1,0:T(8,128)(2,1)} %refs_3_.1, bf16[192,512]{1,0:T(8,128)(2,1)} %refs_4_.1, ...), custom_call_target="tpu_custom_call" | custom-call | tf_op jit(solution)/shard_map/pallas_call | solution.py:575
  31.6 0.8 %shard_map.122 = (bf16[192,1024]{1,0:T(8,128)(2,1)}, f32[192,128]{1,0:T(8,128)}, f32[192,128]{1,0:T(8,128)}) custom-call(bf16[192,1024]{1,0:T(8,128)(2,1)S(1)} %get-tuple-element.6.refs_0_, f32[192,128]{1,0:T(8,128)S(1)} %get-tuple-element.7.refs_1_, f32[192,128]{1,0:T(8,128)S(1)} %get-tuple-element.8.refs_2_), custom_call_target="tpu_custom_call" | custom-call | tf_op jit(solution)/shard_map/pallas_call | solution.py:627
